TPU v7x, 512 devices: a whole 4x4x16 slice. The times are simulated.
512 devices in a mesh: pix: 32 (over z_lo, y), mz: 16 (over z_hi, x, core).
Axes of the slice: x: 4, y: 4, z: 16 (z_hi: 2, z_lo: 8; z = z_hi * 8 + z_lo), core: 2. Of those that a mesh axis runs over, the one named last changes fastest.
Arguments:
- spectra: float32 [512, 393216], P('pix', 'mz'), may hold values from 0.05 to 5
- shifts: int32 [512, 192], P('pix', 'mz'), may hold values from -4 to 3
- fractions: float32 [512, 192], P('pix', 'mz'), may hold values from 0 to 1
- pixel_factors: float32 [512, 32], P('pix'), may hold values from 0.05 to 0.5
- spectral_factors: float32 [32, 393216], P(None, ('mz', 'pix')), may hold values from 0.05 to 0.5
Outputs:
- w_update: float32 [512, 32], P('pix')
- h_update: float32 [32, 393216], P(None, ('mz', 'pix'))
All inputs are finite; a program needn't handle non-finite values.
Results may differ from a plain program's by a relative error of at most 0.0003.
Values sent between devices are 32-bit elements; how exact they have to be, the bound alone decides.
A program may use at most 64 MiB of HBM per device.

v0:
```python
import jax
import jax.numpy as jnp
from jax import lax
from jax.sharding import PartitionSpec as P

SEG = 2048
HALO = 4


EPSILON = 1e-06
exact_mode = lax.Precision.HIGHEST


def padded_2(x, sides, width):
    for axis, dim in sides:
        size, length = (lax.axis_size(axis), x.shape[dim])
        up = [(i, (i + 1) % size) for i in range(size - 1)]
        down = [(j, i) for i, j in up]
        last = lax.slice_in_dim(x, length - width, length, axis=dim)
        leading = lax.slice_in_dim(x, 0, width, axis=dim)
        before = lax.ppermute(last, axis, up)
        after = lax.ppermute(leading, axis, down)
        x = jnp.concatenate([before, x, after], axis=dim)
    return x


def sent_to_all(x, axis):
    copies = jnp.broadcast_to(x, (lax.axis_size(axis), *x.shape))
    return lax.all_to_all(copies, axis, split_axis=0, concat_axis=0, tiled=True)


def taken_together(x, axis):
    return sent_to_all(x, axis).sum(axis=0)


def in_order(pieces, dim):
    lengths = list(pieces.shape[1:])
    lengths[dim] *= pieces.shape[0]
    return jnp.moveaxis(pieces, 0, dim).reshape(lengths)


def gather_directly(x, axis, dim):
    pieces = sent_to_all(x, axis)
    return in_order(pieces, dim)


def split_up(x, dim, size):
    before, after = (x.shape[:dim], x.shape[dim + 1 :])
    return jnp.moveaxis(x.reshape(*before, size, -1, *after), dim, 0)


def summed_on_arrival(x, axis, dim):
    pieces = split_up(x, dim, lax.axis_size(axis))
    arrived = lax.all_to_all(pieces, axis, split_axis=0, concat_axis=0, tiled=True)
    return arrived.sum(axis=0)


def in_one(arrays, axis):
    ends = [0]
    for a in arrays:
        ends.append(ends[-1] + a.size)
    running = taken_together(jnp.concatenate([a.ravel() for a in arrays]), axis)
    return tuple((running[b:e].reshape(a.shape) for a, b, e in zip(arrays, ends, ends[1:])))


def body(spectra, shifts, fractions, pixel_factors, spectral_factors):
    bin_count = spectra.shape[1]
    padded = padded_2(spectra, (("mz", 1),), HALO)
    bin_shift = jnp.repeat(shifts, SEG, axis=1)
    bin_frac = jnp.repeat(fractions, SEG, axis=1)
    lower_term = jnp.zeros_like(spectra)
    upper_term = jnp.zeros_like(spectra)
    for offset in range(-HALO, HALO):
        chosen = bin_shift == offset
        lower_term = jnp.where(
            chosen, padded[:, HALO + offset : HALO + offset + bin_count], lower_term
        )
        upper_term = jnp.where(
            chosen, padded[:, HALO + offset + 1 : HALO + offset + 1 + bin_count], upper_term
        )
    warped = (1.0 - bin_frac) * lower_term + bin_frac * upper_term
    pixel_gram = taken_together(
        jnp.dot(pixel_factors.T, pixel_factors, precision=exact_mode), "pix"
    )
    swapped = lax.all_to_all(warped, "pix", split_axis=1, concat_axis=0, tiled=True)
    all_factors = gather_directly(pixel_factors, "pix", 0)
    numer_share = jnp.dot(all_factors.T, swapped, precision=exact_mode)
    h_update = (
        spectral_factors
        * numer_share
        / (jnp.dot(pixel_gram, spectral_factors, precision=exact_mode) + EPSILON)
    )
    proj_all = jnp.dot(swapped, h_update.T, precision=exact_mode)
    proj_local = summed_on_arrival(proj_all, "pix", 0)
    gram_local = taken_together(jnp.dot(h_update, h_update.T, precision=exact_mode), "pix")
    proj_sum, gram_sum = in_one((proj_local, gram_local), "mz")
    w_update = (
        pixel_factors
        * proj_sum
        / (jnp.dot(pixel_factors, gram_sum, precision=exact_mode) + EPSILON)
    )
    return (w_update, h_update)


def solution(mesh):
    return jax.shard_map(
        body,
        mesh=mesh,
        in_specs=(
            P("pix", "mz"),
            P("pix", "mz"),
            P("pix", "mz"),
            P("pix", None),
            P(None, ("mz", "pix")),
        ),
        out_specs=(P("pix", None), P(None, ("mz", "pix"))),
        check_vma=False,
    )
```

profile of v0, /device:TPU:1, one launch (start us, length us, event | category | flops | bytes accessed | tf_op | source)
XLA Modules:
  0.0 216.0 jit_solution(13427091440214485791)
XLA Ops:
  0.6 0.7 broadcast_in_dim.41
  1.3 0.8 reshape.70
  2.1 16.2 %all-to-all-start.1 = ((f32[32,1,512]{2,1,0:T(1,128)}), f32[32,1,512]{2,1,0:T(1,128)}, u32[]{:S(2)}, u32[]{:S(2)}) async-start(f32[32,1,512]{2,1,0:T(1,128)} %reshape.70), calls=%async_computation.1 | async-start | bytes 131072 | tf_op jit(solution)/shard_map/all_to_all | solution.py:29
  18.4 1.4 fusion.28
  19.8 2.9 %collective-permute-start = (f32[16,4]{1,0:T(8,128)}, f32[16,4]{1,0:T(8,128)}, u32[]{:S(2)}, u32[]{:S(2)}) collective-permute-start(f32[16,4]{1,0:T(8,128)} %get-tuple-element.3), channel_id=1, source_target_pairs={{1,0},{2,1},{3,2},{4,3},{5,4},{6,5},{7,6},{8,7},{9,8},{10,9},{11,1... | collective-permute-start | bytes 776 | tf_op jit(solution)/shard_map/ppermute | solution.py:22
  22.6 3.0 %collective-permute-start.1 = (f32[16,4]{1,0:T(8,128)}, f32[16,4]{1,0:T(8,128)}, u32[]{:S(2)}, u32[]{:S(2)}) collective-permute-start(f32[16,4]{1,0:T(8,128)} %get-tuple-element.2), channel_id=1, source_target_pairs={{0,1},{1,2},{2,3},{3,4},{4,5},{5,6},{6,7},{7,8},{8,9},{9,10},{10,1... | collective-permute-start | bytes 776 | tf_op jit(solution)/shard_map/ppermute | solution.py:21
  25.7 1.5 constant_dynamic-update-slice_fusion.1
  27.2 0.2 broadcast_in_dim.32
  27.4 2.1 copy.20
  29.5 0.2 broadcast_in_dim.33
  29.7 0.3 copy.21
  30.1 0.2 broadcast_in_dim.34
  30.3 1.1 copy.22
  31.4 0.2 broadcast_in_dim.35
  31.6 1.1 copy.23
  32.7 0.2 broadcast_in_dim.36
  32.9 1.1 copy.24
  34.0 0.2 broadcast_in_dim.37
  34.2 1.1 copy.25
  35.3 0.2 broadcast_in_dim.38
  35.5 1.1 copy.26
  36.6 0.2 broadcast_in_dim.39
  36.8 1.1 copy.27
  37.9 0.2 fusion.29
  38.1 0.2 broadcast_in_dim.40
  38.3 1.1 copy.28
  39.4 0.9 broadcast_in_dim.42
  40.3 1.9 reshape.72
  42.3 0.7 constant_dynamic-update-slice_fusion
  43.0 12.3 %all-to-all-start.2 = ((f32[32,1,1024]{2,1,0:T(1,128)}), f32[32,1,1024]{2,1,0:T(1,128)}, u32[]{:S(2)}, u32[]{:S(2)}) async-start(f32[32,1,1024]{2,1,0:T(1,128)} %reshape.72), calls=%async_computation.2 | async-start | bytes 262144 | tf_op jit(solution)/shard_map/all_to_all | solution.py:29
  55.3 5.5 %fusion.4 = f32[16,24576]{1,0:T(8,128)S(1)} fusion(f32[16,24576]{1,0:T(8,128)} %bitcast.54, pred[16,24576]{1,0:T(8,128)(4,1)S(1)} %bitcast.64, f32[16,24580]{1,0:T(8,128)S(1)} %constant_dynamic-update-slice_fusion, pred[16,24576]{1,0:T(8,128)(4,1)} %bitcast.65, pred[16,24576]{1,0:T(8,128)(4,1)} %bitcast.66, pred[16,24576]{1,0:T(8,128)(4,1)} %bitcast.67, ...), kind=kLoop, calls=%fused_computation.9 | loop fusion | flops 9437184 | bytes 14156032 | tf_op jit(solution)/shard_map/add | solution.py:81
  60.8 1.3 copy.30
  62.1 5.3 %all-to-all-done.2 = f32[32,1,1024]{2,1,0:T(1,128)} async-done(((f32[32,1,1024]{2,1,0:T(1,128)}), f32[32,1,1024]{2,1,0:T(1,128)}, u32[]{:S(2)}, u32[]{:S(2)}) %all-to-all-start.2) | async-done | bytes 131104 | tf_op jit(solution)/shard_map/all_to_all | solution.py:29
  67.4 7.1 %all-to-all-start = ((f32[16,32,768]{2,0,1:T(8,128)}), f32[16,32,768]{2,0,1:T(8,128)S(1)}, u32[]{:S(2)}, u32[]{:S(2)}) async-start(f32[16,32,768]{2,0,1:T(8,128)} %bitcast.52), calls=%async_computation | async-start | bytes 3145728 | tf_op jit(solution)/shard_map/all_to_all | solution.py:85
  74.5 0.5 broadcast.42
  75.0 1.6 reduce.1
  76.7 0.1 reshape.71
  76.8 1.9 reduce.2
  78.7 0.2 reshape.73
  78.8 0.1 reduce_sum.36
  78.9 67.5 %all-to-all-done = f32[16,32,768]{2,0,1:T(8,128)S(1)} async-done(((f32[16,32,768]{2,0,1:T(8,128)}), f32[16,32,768]{2,0,1:T(8,128)S(1)}, u32[]{:S(2)}, u32[]{:S(2)}) %all-to-all-start) | async-done | bytes 1572896 | tf_op jit(solution)/shard_map/all_to_all | solution.py:85
  146.4 1.1 fusion.22
  147.5 0.2 fusion.21
  147.7 1.4 fusion.14
  149.1 0.8 reshape.76
  149.9 8.1 %all-to-all-start.3 = ((f32[32,1,512]{2,1,0:T(1,128)}), f32[32,1,512]{2,1,0:T(1,128)S(1)}, u32[]{:S(2)}, u32[]{:S(2)}) async-start(f32[32,1,512]{2,1,0:T(1,128)} %reshape.76), calls=%async_computation.3 | async-start | bytes 131072 | tf_op jit(solution)/shard_map/all_to_all | solution.py:54
  158.0 0.2 fusion.30
  158.3 0.9 reshape.74
  159.2 10.5 %all-to-all-done.3 = f32[32,1,512]{2,1,0:T(1,128)S(1)} async-done(((f32[32,1,512]{2,1,0:T(1,128)}), f32[32,1,512]{2,1,0:T(1,128)S(1)}, u32[]{:S(2)}, u32[]{:S(2)}) %all-to-all-start.3) | async-done | bytes 65568 | tf_op jit(solution)/shard_map/all_to_all | solution.py:54
  169.8 3.9 %all-to-all-start.4 = ((f32[32,1,1024]{2,1,0:T(1,128)}), f32[32,1,1024]{2,1,0:T(1,128)S(1)}, u32[]{:S(2)}, u32[]{:S(2)}) async-start(f32[32,1,1024]{2,1,0:T(1,128)} %reshape.74), calls=%async_computation.4 | async-start | bytes 262144 | tf_op jit(solution)/shard_map/all_to_all | solution.py:29
  173.6 0.8 reduce.4
  174.4 0.1 reshape.77
  174.6 0.1 reshape.64
  174.7 11.1 %all-to-all-done.4 = f32[32,1,1024]{2,1,0:T(1,128)S(1)} async-done(((f32[32,1,1024]{2,1,0:T(1,128)}), f32[32,1,1024]{2,1,0:T(1,128)S(1)}, u32[]{:S(2)}, u32[]{:S(2)}) %all-to-all-start.4) | async-done | bytes 131104 | tf_op jit(solution)/shard_map/all_to_all | solution.py:29
  185.7 1.0 reduce.3
  186.7 0.2 reshape.75
  186.9 0.1 reduce_sum.38
  186.9 0.1 reshape.65
  187.0 0.1 broadcast_in_dim.44
  187.1 27.9 %all_to_all.42 = f32[16,1,1536]{2,1,0:T(1,128)S(1)} all-to-all(f32[16,1,1536]{2,1,0:T(1,128)S(1)} %broadcast_in_dim.44), channel_id=1, replica_groups=mesh['pix'=32,'mz'=16] {'mz'}, dimensions={0} | all-to-all | bytes 196608 | tf_op jit(solution)/shard_map/all_to_all | solution.py:29
  215.0 0.1 reduce_sum.39
  215.1 0.1 reshape.67
  215.2 0.1 reshape.66
  215.2 0.7 fusion.26
  (21 shorter events, 0.2 us)
Async XLA Ops:
  2.1 40.8 %all-to-all-start.1 = ((f32[32,1,512]{2,1,0:T(1,128)}), f32[32,1,512]{2,1,0:T(1,128)}, u32[]{:S(2)}, u32[]{:S(2)}) async-start(f32[32,1,512]{2,1,0:T(1,128)} %reshape.70), calls=%async_computation.1 | async-start | bytes 131072 | tf_op jit(solution)/shard_map/all_to_all | solution.py:29
  19.8 22.5 %collective-permute-start = (f32[16,4]{1,0:T(8,128)}, f32[16,4]{1,0:T(8,128)}, u32[]{:S(2)}, u32[]{:S(2)}) collective-permute-start(f32[16,4]{1,0:T(8,128)} %get-tuple-element.3), channel_id=1, source_target_pairs={{1,0},{2,1},{3,2},{4,3},{5,4},{6,5},{7,6},{8,7},{9,8},{10,9},{11,1... | collective-permute-start | bytes 776 | tf_op jit(solution)/shard_map/ppermute | solution.py:22
  22.6 4.6 %copy-start.4 = (f32[16,12]{1,0:T(8,128)S(1)}, f32[16,12]{1,0:T(8,128)}, u32[]{:S(2)}) copy-start(f32[16,12]{1,0:T(8,128)} %param.7) | copy-start | bytes 2308
  22.6 32.7 %collective-permute-start.1 = (f32[16,4]{1,0:T(8,128)}, f32[16,4]{1,0:T(8,128)}, u32[]{:S(2)}, u32[]{:S(2)}) collective-permute-start(f32[16,4]{1,0:T(8,128)} %get-tuple-element.2), channel_id=1, source_target_pairs={{0,1},{1,2},{2,3},{3,4},{4,5},{5,6},{6,7},{7,8},{8,9},{9,10},{10,1... | collective-permute-start | bytes 776 | tf_op jit(solution)/shard_map/ppermute | solution.py:21
  27.4 2.1 copy-start.5
  35.3 2.6 %copy-start.2 = (f32[16,32]{1,0:T(8,128)S(1)}, f32[16,32]{1,0:T(8,128)}, u32[]{:S(2)}) copy-start(f32[16,32]{1,0:T(8,128)} %param.8) | copy-start | bytes 6148
  37.9 17.4 %copy-start = (f32[16,24576]{1,0:T(8,128)S(1)}, f32[16,24576]{1,0:T(8,128)}, u32[]{:S(2)}) copy-start(f32[16,24576]{1,0:T(8,128)} %param.5) | copy-start | bytes 4718596
  43.0 24.4 %all-to-all-start.2 = ((f32[32,1,1024]{2,1,0:T(1,128)}), f32[32,1,1024]{2,1,0:T(1,128)}, u32[]{:S(2)}, u32[]{:S(2)}) async-start(f32[32,1,1024]{2,1,0:T(1,128)} %reshape.72), calls=%async_computation.2 | async-start | bytes 262144 | tf_op jit(solution)/shard_map/all_to_all | solution.py:29
  67.4 79.0 %all-to-all-start = ((f32[16,32,768]{2,0,1:T(8,128)}), f32[16,32,768]{2,0,1:T(8,128)S(1)}, u32[]{:S(2)}, u32[]{:S(2)}) async-start(f32[16,32,768]{2,0,1:T(8,128)} %bitcast.52), calls=%async_computation | async-start | bytes 3145728 | tf_op jit(solution)/shard_map/all_to_all | solution.py:85
  74.5 71.9 %copy-start.3 = (f32[32,768]{1,0:T(8,128)S(1)}, f32[32,768]{1,0:T(8,128)}, u32[]{:S(2)}) copy-start(f32[32,768]{1,0:T(8,128)} %param.9) | copy-start | bytes 294916
  147.7 11.5 %copy-start.1 = (f32[32,768]{1,0:T(8,128)}, f32[32,768]{1,0:T(8,128)S(1)}, u32[]{:S(2)}) copy-start(f32[32,768]{1,0:T(8,128)S(1)} %fusion.21) | copy-start | bytes 294916
  149.9 19.9 %all-to-all-start.3 = ((f32[32,1,512]{2,1,0:T(1,128)}), f32[32,1,512]{2,1,0:T(1,128)S(1)}, u32[]{:S(2)}, u32[]{:S(2)}) async-start(f32[32,1,512]{2,1,0:T(1,128)} %reshape.76), calls=%async_computation.3 | async-start | bytes 131072 | tf_op jit(solution)/shard_map/all_to_all | solution.py:54
  169.8 16.0 %all-to-all-start.4 = ((f32[32,1,1024]{2,1,0:T(1,128)}), f32[32,1,1024]{2,1,0:T(1,128)S(1)}, u32[]{:S(2)}, u32[]{:S(2)}) async-start(f32[32,1,1024]{2,1,0:T(1,128)} %reshape.74), calls=%async_computation.4 | async-start | bytes 262144 | tf_op jit(solution)/shard_map/all_to_all | solution.py:29
where the time goes:
time: 218 us; the launch traced here: 216 us
  waiting for transfers between devices  94.4 us (43%)
  starting transfers between devices  53.5 us (25%)
  blocking collectives  27.9 us (13%)
  local copies, waits for them, and re-layouts  24.4 us (11%)
  other arithmetic  11 us (5%)
  matrix products  3.86 us (2%)
    all_to_all x1, waiting for transfers between devices, body(): lax.all_to_all(warped, 'pix', split_axis=1, concat_axis=0, tiled=True)  67.5 us
    all_to_all x3, starting transfers between devices, sent_to_all(): return lax.all_to_all(copies, axis, split_axis=0, concat_axis=0, tiled=True)  32.4 us
    all_to_all x1, blocking collectives, sent_to_all(): return lax.all_to_all(copies, axis, split_axis=0, concat_axis=0, tiled=True)  27.9 us
    unnamed x30, local copies, waits for them, and re-layouts  16.6 us
    all_to_all x3, waiting for transfers between devices, sent_to_all(): return lax.all_to_all(copies, axis, split_axis=0, concat_axis=0, tiled=True)  16.3 us
    all_to_all x1, waiting for transfers between devices, summed_on_arrival(): lax.all_to_all(pieces, axis, split_axis=0, concat_axis=0, tiled=True)  10.5 us
    all_to_all x1, starting transfers between devices, summed_on_arrival(): lax.all_to_all(pieces, axis, split_axis=0, concat_axis=0, tiled=True)  8.13 us
    all_to_all x1, starting transfers between devices, body(): lax.all_to_all(warped, 'pix', split_axis=1, concat_axis=0, tiled=True)  7.1 us
  transfers between devices with their start and end apart: 7, of which 4 were waited for; matrix products, arithmetic and copies ran while one was open for 15% of the time, Pallas kernels for 0%

commit v1 on v0

v1 whole, which is shorter than its diff:
```python
import jax
import jax.numpy as jnp
from jax import lax
from jax.experimental import pallas as pl
from jax.experimental.pallas import tpu as pltpu
from jax.sharding import PartitionSpec as P

SEG = 2048
RANK = 32
EPSILON = 1e-06
ROWS = 16
BINS = 24576
SEGS = BINS // SEG
NZ, NY = 8, 4
OWN = 768
PW = 256
NPZ = OWN // PW
NP = NZ * NPZ
GROUP = NY * ROWS
AHEAD = 10
LAGS = (3, 10, 17, 24)
MESH = pl.DeviceIdType.MESH
F32 = jnp.float32
BF16 = jnp.bfloat16
exact_mode = lax.Precision.HIGHEST
NT = (((1,), (1,)), ((), ()))


def halves(v):
    hi = v.astype(BF16)
    return hi, (v - hi.astype(F32)).astype(BF16)


def kernel(
    x_hbm, sh_ref, fr_ref, f_ref, hin_ref, w_ref, hout_ref,
    xp, shb, frb, ws, wg, wgb, cbuf, cout, hbuf, hc, rbuf, fbuf, lhs, gsend, gbuf, acc,
    t1s, t1r, t2s, t2r, t3s, t3r,
    xsem, halo_s, halo_r, f_s, f_r, hc_s, hc_r, g_s, g_r,
    y_s, y_r, c_s, c_r, h_s, h_r, t1_s, t1_r, t2_s, t2_r, t3_s, t3_r,
):
    p, m = lax.axis_index("pix"), lax.axis_index("mz")
    z, y = lax.div(p, NY), lax.rem(p, NY)
    mh, ml = lax.div(m, 8), lax.rem(m, 8)
    low_side = z < NZ // 2
    inner = jnp.where(low_side, p + NY, p - NY)
    outer = jnp.where(low_side, p - NY, p + NY)
    depth = jnp.where(low_side, NZ // 2 - 1 - z, z - NZ // 2)
    center = depth == 0
    slot = jnp.where(center, 1, 0)
    has_outer = depth < NZ // 2 - 1
    lag = jnp.where(
        depth == 0, LAGS[0], jnp.where(depth == 1, LAGS[1], jnp.where(depth == 2, LAGS[2], LAGS[3]))
    )

    def y_dev(r):
        return (z * NY + lax.rem(y + r, NY), m)

    def m_dev(r):
        return (p, mh * 8 + lax.rem(ml + r, 8))

    far = (p, lax.rem(m + 8, 16))

    def rcopy(src, dst, send, recv, dev):
        return pltpu.make_async_remote_copy(
            src_ref=src, dst_ref=dst, send_sem=send, recv_sem=recv, device_id=dev, device_id_type=MESH
        )

    xcopy = pltpu.make_async_copy(x_hbm, xp.at[:, pl.ds(128, BINS)], xsem)
    xcopy.start()

    barrier = pltpu.get_barrier_semaphore()

    def greet(dev):
        pl.semaphore_signal(barrier, inc=1, device_id=dev, device_id_type=MESH)

    for r in range(1, NY):
        greet(y_dev(r))
    for r in range(1, NZ):
        greet((lax.rem(z + r, NZ) * NY + y, m))
    for r in range(1, 8):
        greet(m_dev(r))
    greet(far)

    @pl.when(m == 7)
    def _():
        greet((p, 8))

    @pl.when(m == 8)
    def _():
        greet((p, 7))

    for s in range(SEGS):
        shb[s] = jnp.broadcast_to(sh_ref[:, s : s + 1], (ROWS, 128))
        frb[s] = jnp.broadcast_to(fr_ref[:, s : s + 1], (ROWS, 128))
    acc[...] = jnp.zeros_like(acc)
    fbuf[y] = f_ref[...]

    @pl.when(m == 0)
    def _():
        xp[:, 0:128] = jnp.zeros((ROWS, 128), F32)

    @pl.when(m == 15)
    def _():
        xp[:, 128 + BINS :] = jnp.zeros((ROWS, 128), F32)

    pl.semaphore_wait(barrier, jnp.where((m == 7) | (m == 8), NY + NZ + 7, NY + NZ + 6))

    f_copies = [
        rcopy(f_ref, fbuf.at[y], f_s.at[r - 1], f_r.at[r - 1], y_dev(r)) for r in range(1, NY)
    ]
    for c in f_copies:
        c.start()
    xcopy.wait()

    to_right = rcopy(
        xp.at[:, pl.ds(BINS, 128)], xp.at[:, pl.ds(0, 128)], halo_s.at[0], halo_r.at[0], (p, m + 1)
    )
    to_left = rcopy(
        xp.at[:, pl.ds(128, 128)], xp.at[:, pl.ds(128 + BINS, 128)], halo_s.at[1], halo_r.at[1], (p, m - 1)
    )

    @pl.when(m < 15)
    def _():
        to_right.start()

    @pl.when(m > 0)
    def _():
        to_left.start()

    def h_part(c, j):
        t = z * NPZ + j
        return rcopy(
            hin_ref.at[:, pl.ds(j * PW, PW)], hc.at[t], hc_s.at[c, j], hc_r.at[t], ((3 + c) * NY + y, m)
        )

    for c in range(2):

        @pl.when(z != 3 + c)
        def _():
            for j in range(NPZ):
                h_part(c, j).start()

        @pl.when(z == 3 + c)
        def _():
            for j in range(NPZ):
                hc[z * NPZ + j] = hin_ref[:, j * PW : (j + 1) * PW]

    def piece(i):
        return lax.rem(i + NPZ, NP)

    def y_copy(r, t):
        return rcopy(ws.at[r - 1, t], wg.at[t, y], y_s.at[r - 1], y_r.at[t, r - 1], y_dev(r))

    def warp_send(i):
        t = piece(i)
        zq, j = lax.div(t, NPZ), lax.rem(t, NPZ)
        for r in range(NY):
            b = zq * (NY * OWN) + lax.rem(y + r, NY) * OWN + j * PW
            v = xp[:, pl.ds(pl.multiple_of(b, 128), PW + 256)]
            s = lax.div(b, SEG)
            reps = (PW + 256) // 128
            d = jnp.concatenate([shb[s]] * reps, axis=1)
            f = jnp.concatenate([frb[s]] * (PW // 128), axis=1)
            width = PW + 256
            v = jnp.where(d < 0, pltpu.roll(v, 4, 1), v)
            v = jnp.where((d & 2) != 0, pltpu.roll(v, width - 2, 1), v)
            v = jnp.where((d & 1) != 0, pltpu.roll(v, width - 1, 1), v)
            lower = v[:, 128 : 128 + PW]
            upper = pltpu.roll(v, width - 1, 1)[:, 128 : 128 + PW]
            out = (1.0 - f) * lower + f * upper
            if r == 0:
                wg[t, y] = out
            else:
                ws[r - 1, t] = out
        for r in range(1, NY):
            y_copy(r, t).start()

    def ahead(i, carry):
        warp_send(i)
        return carry

    lax.fori_loop(0, AHEAD, ahead, 0)

    for c in f_copies:
        c.wait_recv()
    fg = fbuf[...].reshape(GROUP, RANK)
    gy = lax.dot_general(fg, fg, (((0,), (0,)), ((), ())), precision=exact_mode, preferred_element_type=F32)
    gsend[...] = gy
    f_hi, f_lo = halves(fg.T)
    lhs[...] = jnp.concatenate([f_hi, f_hi, f_lo], axis=1)

    def g_part(c):
        return rcopy(gsend, gbuf.at[z], g_s.at[c], g_r.at[z], ((3 + c) * NY + y, m))

    for c in range(2):

        @pl.when(z != 3 + c)
        def _():
            g_part(c).start()

        @pl.when(z == 3 + c)
        def _():
            gbuf[z] = gy

    def c_copy(t):
        return rcopy(cout.at[t], cbuf.at[slot, t], c_s, c_r.at[slot, t], (inner, m))

    def c_wait(s, t):
        rcopy(cout.at[t], cbuf.at[s, t], c_s, c_r.at[s, t], (inner, m)).wait_recv()

    def h_copy(t):
        return rcopy(hbuf.at[t], hbuf.at[t], h_s, h_r.at[t], (outer, m))

    def step(i, carry):
        @pl.when(i + AHEAD < NP)
        def _():
            @pl.when(i + AHEAD == NP - NPZ - 1)
            def _():
                @pl.when(m > 0)
                def _():
                    to_right.wait_recv()

                @pl.when(m < 15)
                def _():
                    to_left.wait_recv()

            warp_send(i + AHEAD)

        @pl.when(i < NP)
        def _():
            t = piece(i)
            for r in range(1, NY):
                y_copy(r, t).wait_recv()
            w_hi, w_lo = halves(wg[t].reshape(GROUP, PW))
            both = jnp.concatenate([w_hi, w_lo], axis=0)
            wgb[t] = both
            n = jnp.dot(lhs[...], jnp.concatenate([both, w_hi], axis=0), preferred_element_type=F32)

            @pl.when(has_outer)
            def _():
                c_wait(0, t)
                cout[t] = n + cbuf[0, t]

            @pl.when(jnp.logical_not(has_outer))
            def _():
                cout[t] = n

            c_copy(t).start()

            @pl.when(center)
            def _():
                @pl.when(i == 0)
                def _():
                    for k in range(NZ):

                        @pl.when(z != k)
                        def _():
                            rcopy(gsend, gbuf.at[k], g_s.at[0], g_r.at[k], (inner, m)).wait_recv()

                    total = gbuf[0]
                    for k in range(1, NZ):
                        total = total + gbuf[k]
                    gsum = total
                    gsend_total(gsum)

                @pl.when(lax.div(t, NPZ) != z)
                def _():
                    rcopy(hc.at[t], hc.at[t], hc_s.at[0, 0], hc_r.at[t], (inner, m)).wait_recv()

                own = hc[t]
                bottom = jnp.dot(gbuf[NZ], own, precision=exact_mode, preferred_element_type=F32) + EPSILON
                rbuf[t] = own / bottom

        k = i - lag

        @pl.when((k >= 0) & (k < NP))
        def _():
            t = piece(k)

            @pl.when(center)
            def _():
                c_wait(1, t)
                hbuf[t] = rbuf[t] * (cout[t] + cbuf[1, t])

            @pl.when(jnp.logical_not(center))
            def _():
                h_copy(t).wait_recv()

            @pl.when(has_outer)
            def _():
                h_copy(t).start()

            h = hbuf[t]
            h_hi, h_lo = halves(h)
            right = jnp.concatenate([h_hi, h_lo], axis=0)
            left = jnp.concatenate([wgb[t], right], axis=0)
            acc[...] += lax.dot_general(left, right, NT, preferred_element_type=F32)

            @pl.when(lax.div(t, NPZ) == z)
            def _():
                hout_ref[:, pl.ds(pl.multiple_of(lax.rem(t, NPZ) * PW, 128), PW)] = h

        return carry

    def gsend_total(total):
        gbuf[NZ] = total

    lax.fori_loop(0, NP + LAGS[-1], step, 0)

    both = acc[:, 0:RANK] + acc[:, RANK : 2 * RANK]
    proj = both[0:GROUP] + both[GROUP : 2 * GROUP]
    base = 2 * GROUP
    gram = both[base : base + RANK] + both[base + RANK : base + 2 * RANK]
    for k in range(NY):
        t1s[k] = jnp.concatenate(
            [proj[k * ROWS : (k + 1) * ROWS], gram[0:ROWS], gram[ROWS : 2 * ROWS], jnp.zeros((ROWS, 32), F32)],
            axis=1,
        )
    t1_copies = [
        rcopy(t1s.at[lax.rem(y + r, NY)], t1r.at[y], t1_s.at[r - 1], t1_r.at[r - 1], y_dev(r))
        for r in range(1, NY)
    ]
    for c in t1_copies:
        c.start()
    t1r[y] = t1s[y]
    for c in t1_copies:
        c.wait_recv()
    part = t1r[0]
    for k in range(1, NY):
        part = part + t1r[k]
    t2s[...] = part
    t2_copies = [
        rcopy(t2s, t2r.at[ml], t2_s.at[r - 1], t2_r.at[r - 1], m_dev(r)) for r in range(1, 8)
    ]
    for c in t2_copies:
        c.start()
    t2r[ml] = part
    for c in t2_copies:
        c.wait_recv()
    part = t2r[0]
    for k in range(1, 8):
        part = part + t2r[k]
    t3s[...] = part
    t3_copy = rcopy(t3s, t3r, t3_s, t3_r, far)
    t3_copy.start()
    t3_copy.wait_recv()
    total = part + t3r[...]
    gram_sum = jnp.concatenate([total[:, 32:64], total[:, 64:96]], axis=0)
    f = f_ref[...]
    bottom = jnp.dot(f, gram_sum, precision=exact_mode, preferred_element_type=F32) + EPSILON
    w_ref[...] = f * total[:, 0:32] / bottom

    for c in f_copies + t1_copies + t2_copies + [t3_copy]:
        c.wait_send()

    @pl.when(m < 15)
    def _():
        to_right.wait_send()

    @pl.when(m > 0)
    def _():
        to_left.wait_send()

    for c in range(2):

        @pl.when(z != 3 + c)
        def _():
            for j in range(NPZ):
                h_part(c, j).wait_send()
            g_part(c).wait_send()

    for r in range(1, NY):
        rcopy(ws.at[r - 1], ws.at[r - 1], y_s.at[r - 1], y_s.at[r - 1], y_dev(r)).wait_send()
    rcopy(cout, cout, c_s, c_s, (inner, m)).wait_send()

    @pl.when(has_outer)
    def _():
        rcopy(hbuf, hbuf, h_s, h_s, (outer, m)).wait_send()


def body(spectra, shifts, fractions, pixel_factors, spectral_factors):
    vmem = pl.BlockSpec(memory_space=pltpu.VMEM)
    dma = pltpu.SemaphoreType.DMA
    return pl.pallas_call(
        kernel,
        out_shape=(
            jax.ShapeDtypeStruct((ROWS, RANK), F32),
            jax.ShapeDtypeStruct((RANK, OWN), F32),
        ),
        in_specs=[pl.BlockSpec(memory_space=pl.ANY)] + [vmem] * 4,
        out_specs=(vmem, vmem),
        scratch_shapes=[
            pltpu.VMEM((ROWS, BINS + 256), F32),
            pltpu.VMEM((SEGS, ROWS, 128), jnp.int32),
            pltpu.VMEM((SEGS, ROWS, 128), F32),
            pltpu.VMEM((NY - 1, NP, ROWS, PW), F32),
            pltpu.VMEM((NP, NY, ROWS, PW), F32),
            pltpu.VMEM((NP, 2 * GROUP, PW), BF16),
            pltpu.VMEM((2, NP, RANK, PW), F32),
            pltpu.VMEM((NP, RANK, PW), F32),
            pltpu.VMEM((NP, RANK, PW), F32),
            pltpu.VMEM((NP, RANK, PW), F32),
            pltpu.VMEM((NP, RANK, PW), F32),
            pltpu.VMEM((NY, ROWS, RANK), F32),
            pltpu.VMEM((RANK, 3 * GROUP), BF16),
            pltpu.VMEM((RANK, RANK), F32),
            pltpu.VMEM((NZ + 1, RANK, RANK), F32),
            pltpu.VMEM((2 * GROUP + 2 * RANK, 2 * RANK), F32),
            pltpu.VMEM((NY, ROWS, 128), F32),
            pltpu.VMEM((NY, ROWS, 128), F32),
            pltpu.VMEM((ROWS, 128), F32),
            pltpu.VMEM((8, ROWS, 128), F32),
            pltpu.VMEM((ROWS, 128), F32),
            pltpu.VMEM((ROWS, 128), F32),
            dma(()),
            dma((2,)),
            dma((2,)),
            dma((NY - 1,)),
            dma((NY - 1,)),
            dma((2, NPZ)),
            dma((NP,)),
            dma((2,)),
            dma((NZ,)),
            dma((NY - 1,)),
            dma((NP, NY - 1)),
            dma(()),
            dma((2, NP)),
            dma(()),
            dma((NP,)),
            dma((NY - 1,)),
            dma((NY - 1,)),
            dma((7,)),
            dma((7,)),
            dma(()),
            dma(()),
        ],
        compiler_params=pltpu.CompilerParams(
            collective_id=0, has_side_effects=True, vmem_limit_bytes=48 * 1024 * 1024
        ),
    )(spectra, shifts, fractions, pixel_factors, spectral_factors)


def solution(mesh):
    return jax.shard_map(
        body,
        mesh=mesh,
        in_specs=(
            P("pix", "mz"),
            P("pix", "mz"),
            P("pix", "mz"),
            P("pix", None),
            P(None, ("mz", "pix")),
        ),
        out_specs=(P("pix", None), P(None, ("mz", "pix"))),
        check_vma=False,
    )
```

time: 218 us -> 92.3 us (0.42)
  waiting for transfers between devices: 94.4 us -> 0 us
  Pallas kernels: 0 us -> 85.7 us
  starting transfers between devices: 53.5 us -> 0 us
  blocking collectives: 27.9 us -> 0 us
  local copies, waits for them, and re-layouts: 24.4 us -> 5.62 us
  other arithmetic: 11 us -> 0 us
  matrix products: 3.86 us -> 0 us
    all_to_all x5 -> x0, waiting for transfers between devices: 94.4 us -> none  [the longest x1 67.5 us: body(): lax.all_to_all(warped, 'pix', split_axis=1, concat_axis=0, tiled=True)]
    pallas_call x0 -> x1, Pallas kernels: none -> 85.7 us  [body(): pl.pallas_call(kernel, out_shape=(jax.ShapeDtypeStruct((ROWS, RANK), F32)...]
    all_to_all x5 -> x0, starting transfers between devices: 47.6 us -> none  [the longest x3 32.4 us: sent_to_all(): return lax.all_to_all(copies, axis, split_axis=0, concat_axis=0, tiled=True)]
    all_to_all x1 -> x0, blocking collectives: 27.9 us -> none  [sent_to_all(): return lax.all_to_all(copies, axis, split_axis=0, concat_axis=0, tiled=True)]
    unnamed x30 -> x12, local copies, waits for them, and re-layouts: 16.6 us -> 5.62 us
    ppermute x2 -> x0, starting transfers between devices: 5.87 us -> none  [the longest x1 3.02 us: padded_2(): before = lax.ppermute(last, axis, up)]
    add x1 -> x0, other arithmetic: 5.47 us -> none  [body(): warped = (1.0 - bin_frac) * lower_term + bin_frac * upper_term]
    all_to_all x4 -> x0, other arithmetic: 5.25 us -> none  [the longest x3 4.45 us: sent_to_all(): return lax.all_to_all(copies, axis, split_axis=0, concat_axis=0, tiled=True)]
  transfers between devices with their start and end apart: 7 -> 0, of which waited for: 4 -> 0; matrix products, arithmetic and copies ran while one was open for 15% -> 0% of each run, Pallas kernels for 0% -> 0%
where the time goes in v1:
time: 92.3 us; the launch traced here: 92 us
  Pallas kernels  85.7 us (93%)
  local copies, waits for them, and re-layouts  5.62 us (6%)
    pallas_call x1, Pallas kernels, body(): pl.pallas_call(kernel, out_shape=(jax.ShapeDtypeStruct((ROWS, RANK), F32)...  85.7 us
    unnamed x12, local copies, waits for them, and re-layouts  5.62 us

profile of v1, /device:TPU:1, one launch (start us, length us, event | category | flops | bytes accessed | tf_op | source)
XLA Modules:
  0.0 92.0 jit_solution(12245941087777969002)
XLA Ops:
  0.6 0.0 copy-start
  0.6 1.4 %copy-done = f32[16,24576]{1,0:T(8,128)S(1)} copy-done((f32[16,24576]{1,0:T(8,128)S(1)}, f32[16,24576]{1,0:T(8,128)}, u32[]{:S(2)}) %copy-start) | copy-done | bytes 1572888
  2.0 0.0 copy-start.1
  2.0 0.9 copy-done.1
  2.9 0.0 copy-start.2
  2.9 0.7 copy-done.2
  3.6 0.0 copy-start.3
  3.6 0.7 copy-done.3
  4.3 0.0 copy-start.4
  4.3 0.7 copy-done.4
  5.0 85.7 %shard_map.68 = (f32[16,32]{1,0:T(8,128)S(1)}, f32[32,768]{1,0:T(8,128)S(1)}) custom-call(f32[16,24576]{1,0:T(8,128)S(1)} %copy-done, s32[16,12]{1,0:T(8,128)S(1)} %copy-done.2, f32[16,12]{1,0:T(8,128)S(1)} %copy-done.3, f32[16,32]{1,0:T(8,128)S(1)} %copy-done.4, f32[32,768]{1,0:T(8,128)S(1)} %copy-done.1), custom_call_target="tpu_custom_call" | custom-call | tf_op jit(solution)/shard_map/pallas_call | solution.py:384
  90.8 0.6 copy.9
  91.4 0.6 copy.10
Async XLA Ops:
  0.6 1.4 %copy-start = (f32[16,24576]{1,0:T(8,128)S(1)}, f32[16,24576]{1,0:T(8,128)}, u32[]{:S(2)}) copy-start(f32[16,24576]{1,0:T(8,128)} %x_hbm.1) | copy-start | bytes 4718596
  2.0 0.9 copy-start.1
  2.9 0.7 copy-start.2
  3.6 0.7 copy-start.3
  4.3 0.7 copy-start.4

commit v2 on v1

v2 whole, which is shorter than its diff:
```python
import jax
import jax.numpy as jnp
from jax import lax
from jax.experimental import pallas as pl
from jax.experimental.pallas import tpu as pltpu
from jax.sharding import PartitionSpec as P

SEG = 2048
RANK = 32
EPSILON = 1e-06
ROWS = 16
BINS = 24576
SEGS = BINS // SEG
NZ, NY = 8, 4
OWN = 768
PW = 256
NPZ = OWN // PW
NP = NZ * NPZ
GROUP = NY * ROWS
FIRST = 14
AHEAD = 10
LAGS = (5, 13, 21, 24)
PEERS = 32
MESH = pl.DeviceIdType.MESH
F32 = jnp.float32
BF16 = jnp.bfloat16
exact_mode = lax.Precision.HIGHEST
NT = (((1,), (1,)), ((), ()))


def halves(v):
    hi = v.astype(BF16)
    return hi, (v - hi.astype(F32)).astype(BF16)


def kernel(
    x_hbm, sh_hbm, fr_hbm, f_hbm, hin_hbm, w_ref, hout_ref,
    sh_ref, fr_ref, f_ref, hin_ref,
    xp, shb, frb, ws, wg, wgb, cbuf, cout, hbuf, hc, rbuf, fbuf, lhs, gsend, gbuf, acc,
    t1s, t1r, t3s, t3r,
    xsem, halo_s, halo_r, f_s, f_r, hc_s, hc_r, g_s, g_r,
    y_s, y_r, c_s, c_r, h_s, h_r, t1_s, t1_r, t3_s, t3_r,
):
    p, m = lax.axis_index("pix"), lax.axis_index("mz")
    z, y = lax.div(p, NY), lax.rem(p, NY)
    mh, ml = lax.div(m, 8), lax.rem(m, 8)
    low_side = z < NZ // 2
    inner = jnp.where(low_side, p + NY, p - NY)
    outer = jnp.where(low_side, p - NY, p + NY)
    depth = jnp.where(low_side, NZ // 2 - 1 - z, z - NZ // 2)
    center = depth == 0
    slot = jnp.where(center, 1, 0)
    has_outer = depth < NZ // 2 - 1
    lag = jnp.where(
        depth == 0, LAGS[0], jnp.where(depth == 1, LAGS[1], jnp.where(depth == 2, LAGS[2], LAGS[3]))
    )

    def y_dev(r):
        return (z * NY + lax.rem(y + r, NY), m)

    def m_dev(r):
        return (p, mh * 8 + lax.rem(ml + r, 8))

    far = (p, lax.rem(m + 8, 16))

    def rcopy(src, dst, send, recv, dev):
        return pltpu.make_async_remote_copy(
            src_ref=src, dst_ref=dst, send_sem=send, recv_sem=recv, device_id=dev, device_id_type=MESH
        )

    loads = [
        pltpu.make_async_copy(a, b, xsem.at[k])
        for k, (a, b) in enumerate(
            (
                (sh_hbm, sh_ref),
                (fr_hbm, fr_ref),
                (x_hbm, xp.at[:, pl.ds(128, BINS)]),
                (f_hbm, f_ref),
                (hin_hbm, hin_ref),
            )
        )
    ]
    for c in loads:
        c.start()

    barrier = pltpu.get_barrier_semaphore()

    def greet(dev):
        pl.semaphore_signal(barrier, inc=1, device_id=dev, device_id_type=MESH)

    def plane_dev(k):
        return (
            z * NY + lax.rem(y + lax.div(k, 8), NY),
            mh * 8 + lax.rem(ml + lax.rem(k, 8), 8),
        )

    for k in range(1, PEERS):
        greet(plane_dev(k))
    half = lax.div(z, NZ // 2) * (NZ // 2)
    for r in range(1, NZ // 2):
        greet(((half + lax.rem(z + r, NZ // 2)) * NY + y, m))
    greet(far)

    @pl.when(center)
    def _():
        greet((inner, m))

    @pl.when(m == 7)
    def _():
        greet((p, 8))

    @pl.when(m == 8)
    def _():
        greet((p, 7))

    acc[...] = jnp.zeros_like(acc)

    @pl.when(m == 0)
    def _():
        xp[:, 0:128] = jnp.zeros((ROWS, 128), F32)

    @pl.when(m == 15)
    def _():
        xp[:, 128 + BINS :] = jnp.zeros((ROWS, 128), F32)

    loads[0].wait()
    loads[1].wait()
    for s in range(SEGS):
        shb[s] = jnp.broadcast_to(sh_ref[:, s : s + 1], (ROWS, 128))
        frb[s] = jnp.broadcast_to(fr_ref[:, s : s + 1], (ROWS, 128))

    with jax.named_scope("xwait"):
        loads[2].wait()

    def piece(i):
        return lax.rem(i + NPZ, NP)

    def y_copy(r, t):
        return rcopy(ws.at[r - 1, t], wg.at[t, y], y_s.at[r - 1], y_r.at[t, r - 1], y_dev(r))

    def warp(i):
        t = piece(i)
        zq, j = lax.div(t, NPZ), lax.rem(t, NPZ)
        for r in range(NY):
            b = zq * (NY * OWN) + lax.rem(y + r, NY) * OWN + j * PW
            v = xp[:, pl.ds(pl.multiple_of(b, 128), PW + 256)]
            s = lax.div(b, SEG)
            reps = (PW + 256) // 128
            d = jnp.concatenate([shb[s]] * reps, axis=1)
            f = jnp.concatenate([frb[s]] * (PW // 128), axis=1)
            width = PW + 256
            v = jnp.where(d < 0, pltpu.roll(v, 4, 1), v)
            v = jnp.where((d & 2) != 0, pltpu.roll(v, width - 2, 1), v)
            v = jnp.where((d & 1) != 0, pltpu.roll(v, width - 1, 1), v)
            lower = v[:, 128 : 128 + PW]
            upper = pltpu.roll(v, width - 1, 1)[:, 128 : 128 + PW]
            out = (1.0 - f) * lower + f * upper
            if r == 0:
                wg[t, y] = out
            else:
                ws[r - 1, t] = out

    def send(i):
        t = piece(i)
        for r in range(1, NY):
            y_copy(r, t).start()

    def warp_early(i, carry):
        warp(i)
        return carry

    def send_early(i, carry):
        send(i)
        return carry

    with jax.named_scope("warps"):
        lax.fori_loop(0, FIRST, warp_early, 0)
    loads[3].wait()
    loads[4].wait()
    fbuf[y] = f_ref[...]
    with jax.named_scope("barrier"):
        pl.semaphore_wait(
            barrier,
            PEERS + NZ // 2 - 1 + jnp.where(center, 1, 0) + jnp.where((m == 7) | (m == 8), 1, 0),
        )

    f_copies = [
        rcopy(f_ref, fbuf.at[y], f_s.at[r - 1], f_r.at[r - 1], y_dev(r)) for r in range(1, NY)
    ]
    for c in f_copies:
        c.start()
    lax.fori_loop(0, FIRST, send_early, 0)

    to_right = rcopy(
        xp.at[:, pl.ds(BINS, 128)], xp.at[:, pl.ds(0, 128)], halo_s.at[0], halo_r.at[0], (p, m + 1)
    )
    to_left = rcopy(
        xp.at[:, pl.ds(128, 128)], xp.at[:, pl.ds(128 + BINS, 128)], halo_s.at[1], halo_r.at[1], (p, m - 1)
    )

    @pl.when(m < 15)
    def _():
        to_right.start()

    @pl.when(m > 0)
    def _():
        to_left.start()

    near = jnp.where(low_side, NZ // 2 - 1, NZ // 2)

    def h_part(j):
        t = z * NPZ + j
        dev = (jnp.where(center, inner, near * NY + y), m)
        return rcopy(hin_ref.at[:, pl.ds(j * PW, PW)], hc.at[t], hc_s, hc_r.at[t], dev)

    def h_relay(t):
        return rcopy(hc.at[t], hc.at[t], hc_s, hc_r.at[t], (inner, m))

    for j in range(NPZ):
        h_part(j).start()

    @pl.when(center)
    def _():
        for j in range(NPZ):
            hc[z * NPZ + j] = hin_ref[:, j * PW : (j + 1) * PW]

    with jax.named_scope("fwait"):
        for c in f_copies:
            c.wait_recv()
    fg = fbuf[...].reshape(GROUP, RANK)
    gy = lax.dot_general(fg, fg, (((0,), (0,)), ((), ())), precision=exact_mode, preferred_element_type=F32)
    f_hi, f_lo = halves(fg.T)
    lhs[...] = jnp.concatenate([f_hi, f_hi, f_lo], axis=1)

    g_half = rcopy(gsend, gbuf.at[z], g_s, g_r.at[z], (near * NY + y, m))
    g_other = rcopy(gsend, gbuf.at[NZ], g_s, g_r.at[NZ], (inner, m))

    def outward(k):
        return jnp.where(low_side, NZ // 2 - 1 - k, NZ // 2 + k)

    @pl.when(jnp.logical_not(center))
    def _():
        gsend[...] = gy
        g_half.start()

    @pl.when(center)
    def _():
        total = gy
        for k in range(1, NZ // 2):
            zk = outward(k)
            rcopy(gsend, gbuf.at[zk], g_s, g_r.at[zk], (inner, m)).wait_recv()
            total = total + gbuf[zk]
        gsend[...] = total
        g_other.start()
        with jax.named_scope("relay"):
            for k in range(1, NZ // 2):
                for j in range(NPZ):
                    t = outward(k) * NPZ + j
                    h_relay(t).wait_recv()
                    h_relay(t).start()
        g_other.wait_recv()
        gbuf[NZ + 1] = total + gbuf[NZ]

    def c_copy(t):
        return rcopy(cout.at[t], cbuf.at[slot, t], c_s, c_r.at[slot, t], (inner, m))

    def c_wait(s, t):
        rcopy(cout.at[t], cbuf.at[s, t], c_s, c_r.at[s, t], (inner, m)).wait_recv()

    def h_copy(t):
        return rcopy(hbuf.at[t], hbuf.at[t], h_s, h_r.at[t], (outer, m))

    def step(i, carry):
        @pl.when((i >= FIRST - AHEAD) & (i + AHEAD < NP))
        def _():
            @pl.when(i + AHEAD == NP - NPZ - 1)
            def _():
                @pl.when(m > 0)
                def _():
                    to_right.wait_recv()

                @pl.when(m < 15)
                def _():
                    to_left.wait_recv()

            warp(i + AHEAD)
            send(i + AHEAD)

        @pl.when(i < NP)
        def _():
            t = piece(i)
            with jax.named_scope("ywait"):
                for r in range(1, NY):
                    y_copy(r, t).wait_recv()
            w_hi, w_lo = halves(wg[t].reshape(GROUP, PW))
            both = jnp.concatenate([w_hi, w_lo], axis=0)
            wgb[t] = both
            n = jnp.dot(lhs[...], jnp.concatenate([both, w_hi], axis=0), preferred_element_type=F32)

            @pl.when(has_outer)
            def _():
                with jax.named_scope("cwait"):
                    c_wait(0, t)
                cout[t] = n + cbuf[0, t]

            @pl.when(jnp.logical_not(has_outer))
            def _():
                cout[t] = n

            c_copy(t).start()

            @pl.when(center)
            def _():
                @pl.when(lax.div(t, NPZ * (NZ // 2)) != lax.div(z, NZ // 2))
                def _():
                    with jax.named_scope("hcwait"):
                        h_relay(t).wait_recv()

                own = hc[t]
                bottom = jnp.dot(gbuf[NZ + 1], own, precision=exact_mode, preferred_element_type=F32) + EPSILON
                rbuf[t] = own / bottom

        k = i - lag

        @pl.when((k >= 0) & (k < NP))
        def _():
            t = piece(k)

            @pl.when(center)
            def _():
                with jax.named_scope("xcwait"):
                    c_wait(1, t)
                hbuf[t] = rbuf[t] * (cout[t] + cbuf[1, t])

            @pl.when(jnp.logical_not(center))
            def _():
                with jax.named_scope("hwait"):
                    h_copy(t).wait_recv()

            @pl.when(has_outer)
            def _():
                h_copy(t).start()

            h = hbuf[t]
            h_hi, h_lo = halves(h)
            right = jnp.concatenate([h_hi, h_lo], axis=0)
            left = jnp.concatenate([wgb[t], right], axis=0)
            acc[...] += lax.dot_general(left, right, NT, preferred_element_type=F32)

            @pl.when(lax.div(t, NPZ) == z)
            def _():
                hout_ref[:, pl.ds(pl.multiple_of(lax.rem(t, NPZ) * PW, 128), PW)] = h

        return carry

    lax.fori_loop(0, NP + LAGS[-1], step, 0)

    both = acc[:, 0:RANK] + acc[:, RANK : 2 * RANK]
    proj = both[0:GROUP] + both[GROUP : 2 * GROUP]
    base = 2 * GROUP
    gram = both[base : base + RANK] + both[base + RANK : base + 2 * RANK]
    for k in range(NY):
        t1s[k] = jnp.concatenate(
            [proj[k * ROWS : (k + 1) * ROWS], gram[0:ROWS], gram[ROWS : 2 * ROWS], jnp.zeros((ROWS, 32), F32)],
            axis=1,
        )

    me = y * 8 + ml

    def t_copy(k):
        return rcopy(
            t1s.at[lax.rem(y + lax.div(k, 8), NY)], t1r.at[me], t1_s.at[k], t1_r.at[k], plane_dev(k)
        )

    def t_start(k, carry):
        t_copy(k).start()
        return carry

    def t_recv(k, carry):
        t_copy(k).wait_recv()
        return carry

    def t_sent(k, carry):
        t_copy(k).wait_send()
        return carry

    lax.fori_loop(1, PEERS, t_start, 0)
    t1r[me] = t1s[y]
    with jax.named_scope("t1wait"):
        lax.fori_loop(1, PEERS, t_recv, 0)
    part = t1r[0]
    for k in range(1, PEERS):
        part = part + t1r[k]
    t3s[...] = part
    t3_copy = rcopy(t3s, t3r, t3_s, t3_r, far)
    t3_copy.start()
    with jax.named_scope("t3wait"):
        t3_copy.wait_recv()
    total = part + t3r[...]
    gram_sum = jnp.concatenate([total[:, 32:64], total[:, 64:96]], axis=0)
    f = f_ref[...]
    bottom = jnp.dot(f, gram_sum, precision=exact_mode, preferred_element_type=F32) + EPSILON
    w_ref[...] = f * total[:, 0:32] / bottom

    for c in f_copies + [t3_copy]:
        c.wait_send()
    lax.fori_loop(1, PEERS, t_sent, 0)

    @pl.when(m < 15)
    def _():
        to_right.wait_send()

    @pl.when(m > 0)
    def _():
        to_left.wait_send()

    g_half.wait_send()
    def hc_sent(pieces):
        part = hc.at[pl.ds(0, pieces)]
        rcopy(part, part, hc_s, hc_s, (inner, m)).wait_send()

    @pl.when(center)
    def _():
        hc_sent(NPZ * (NZ // 2))

    @pl.when(jnp.logical_not(center))
    def _():
        hc_sent(NPZ)

    for r in range(1, NY):
        rcopy(ws.at[r - 1], ws.at[r - 1], y_s.at[r - 1], y_s.at[r - 1], y_dev(r)).wait_send()
    rcopy(cout, cout, c_s, c_s, (inner, m)).wait_send()

    @pl.when(has_outer)
    def _():
        rcopy(hbuf, hbuf, h_s, h_s, (outer, m)).wait_send()


def body(spectra, shifts, fractions, pixel_factors, spectral_factors):
    vmem = pl.BlockSpec(memory_space=pltpu.VMEM)
    dma = pltpu.SemaphoreType.DMA
    return pl.pallas_call(
        kernel,
        out_shape=(
            jax.ShapeDtypeStruct((ROWS, RANK), F32),
            jax.ShapeDtypeStruct((RANK, OWN), F32),
        ),
        in_specs=[pl.BlockSpec(memory_space=pltpu.HBM)] * 5,
        out_specs=(vmem, vmem),
        scratch_shapes=[
            pltpu.VMEM((ROWS, SEGS), jnp.int32),
            pltpu.VMEM((ROWS, SEGS), F32),
            pltpu.VMEM((ROWS, RANK), F32),
            pltpu.VMEM((RANK, OWN), F32),
            pltpu.VMEM((ROWS, BINS + 256), F32),
            pltpu.VMEM((SEGS, ROWS, 128), jnp.int32),
            pltpu.VMEM((SEGS, ROWS, 128), F32),
            pltpu.VMEM((NY - 1, NP, ROWS, PW), F32),
            pltpu.VMEM((NP, NY, ROWS, PW), F32),
            pltpu.VMEM((NP, 2 * GROUP, PW), BF16),
            pltpu.VMEM((2, NP, RANK, PW), F32),
            pltpu.VMEM((NP, RANK, PW), F32),
            pltpu.VMEM((NP, RANK, PW), F32),
            pltpu.VMEM((NP, RANK, PW), F32),
            pltpu.VMEM((NP, RANK, PW), F32),
            pltpu.VMEM((NY, ROWS, RANK), F32),
            pltpu.VMEM((RANK, 3 * GROUP), BF16),
            pltpu.VMEM((RANK, RANK), F32),
            pltpu.VMEM((NZ + 2, RANK, RANK), F32),
            pltpu.VMEM((2 * GROUP + 2 * RANK, 2 * RANK), F32),
            pltpu.VMEM((NY, ROWS, 128), F32),
            pltpu.VMEM((PEERS, ROWS, 128), F32),
            pltpu.VMEM((ROWS, 128), F32),
            pltpu.VMEM((ROWS, 128), F32),
            dma((5,)),
            dma((2,)),
            dma((2,)),
            dma((NY - 1,)),
            dma((NY - 1,)),
            dma(()),
            dma((NP,)),
            dma(()),
            dma((NZ + 1,)),
            dma((NY - 1,)),
            dma((NP, NY - 1)),
            dma(()),
            dma((2, NP)),
            dma(()),
            dma((NP,)),
            dma((PEERS,)),
            dma((PEERS,)),
            dma(()),
            dma(()),
        ],
        compiler_params=pltpu.CompilerParams(
            collective_id=0, has_side_effects=True, vmem_limit_bytes=48 * 1024 * 1024
        ),
    )(spectra, shifts, fractions, pixel_factors, spectral_factors)


def solution(mesh):
    return jax.shard_map(
        body,
        mesh=mesh,
        in_specs=(
            P("pix", "mz"),
            P("pix", "mz"),
            P("pix", "mz"),
            P("pix", None),
            P(None, ("mz", "pix")),
        ),
        out_specs=(P("pix", None), P(None, ("mz", "pix"))),
        check_vma=False,
    )
```

time: 92.3 us -> 86.2 us (0.934)
  Pallas kernels: 85.7 us -> 79.6 us
    pallas_call x1, Pallas kernels: 85.7 us -> 79.6 us  [body(): pl.pallas_call(kernel, out_shape=(jax.ShapeDtypeStruct((ROWS, RANK), F32)...]
where the time goes in v2:
time: 86.2 us; the launch traced here: 85.9 us
  Pallas kernels  79.6 us (92%)
  local copies, waits for them, and re-layouts  5.62 us (7%)
    pallas_call x1, Pallas kernels, body(): pl.pallas_call(kernel, out_shape=(jax.ShapeDtypeStruct((ROWS, RANK), F32)...  79.6 us
    unnamed x12, local copies, waits for them, and re-layouts  5.62 us

profile of v2, /device:TPU:1, one launch (start us, length us, event | category | flops | bytes accessed | tf_op | source)
XLA Modules:
  0.0 85.9 jit_solution(7643515979898329049)
XLA Ops:
  0.6 0.0 copy-start
  0.6 1.4 %copy-done = f32[16,24576]{1,0:T(8,128)S(1)} copy-done((f32[16,24576]{1,0:T(8,128)S(1)}, f32[16,24576]{1,0:T(8,128)}, u32[]{:S(2)}) %copy-start) | copy-done | bytes 1572888
  2.0 0.0 copy-start.1
  2.0 0.9 %copy-done.1 = f32[32,768]{1,0:T(8,128)S(1)} copy-done((f32[32,768]{1,0:T(8,128)S(1)}, f32[32,768]{1,0:T(8,128)}, u32[]{:S(2)}) %copy-start.1) | copy-done | bytes 98328
  2.9 0.0 copy-start.2
  2.9 0.7 copy-done.2
  3.6 0.0 copy-start.3
  3.6 0.7 copy-done.3
  4.3 0.0 copy-start.4
  4.3 0.7 copy-done.4
  5.0 79.6 %shard_map.68 = (f32[16,32]{1,0:T(8,128)S(1)}, f32[32,768]{1,0:T(8,128)S(1)}) custom-call(f32[16,24576]{1,0:T(8,128)S(1)} %copy-done, s32[16,12]{1,0:T(8,128)S(1)} %copy-done.2, f32[16,12]{1,0:T(8,128)S(1)} %copy-done.3, f32[16,32]{1,0:T(8,128)S(1)} %copy-done.4, f32[32,768]{1,0:T(8,128)S(1)} %copy-done.1), custom_call_target="tpu_custom_call" | custom-call | tf_op jit(solution)/shard_map/pallas_call | solution.py:442
  84.6 0.6 copy.9
  85.2 0.6 copy.10
Async XLA Ops:
  0.6 1.4 %copy-start = (f32[16,24576]{1,0:T(8,128)S(1)}, f32[16,24576]{1,0:T(8,128)}, u32[]{:S(2)}) copy-start(f32[16,24576]{1,0:T(8,128)} %x_hbm.1) | copy-start | bytes 4718596
  2.0 0.9 %copy-start.1 = (f32[32,768]{1,0:T(8,128)S(1)}, f32[32,768]{1,0:T(8,128)}, u32[]{:S(2)}) copy-start(f32[32,768]{1,0:T(8,128)} %hin_hbm.1) | copy-start | bytes 294916
  2.9 0.7 copy-start.2
  3.6 0.7 copy-start.3
  4.3 0.7 copy-start.4

commit v3 on v2

--- a/solution.py
+++ b/solution.py
@@ -17,9 +17,10 @@
 NPZ = OWN // PW
 NP = NZ * NPZ
 GROUP = NY * ROWS
-FIRST = 14
-AHEAD = 10
 LAGS = (5, 13, 21, 24)
+CHUNK = 1024
+GROUP_BINS = NY * OWN
+EARLY = 6
 PEERS = 32
 MESH = pl.DeviceIdType.MESH
 F32 = jnp.float32
@@ -68,19 +69,20 @@
             src_ref=src, dst_ref=dst, send_sem=send, recv_sem=recv, device_id=dev, device_id_type=MESH
         )
 
-    loads = [
+    small = [
         pltpu.make_async_copy(a, b, xsem.at[k])
         for k, (a, b) in enumerate(
-            (
-                (sh_hbm, sh_ref),
-                (fr_hbm, fr_ref),
-                (x_hbm, xp.at[:, pl.ds(128, BINS)]),
-                (f_hbm, f_ref),
-                (hin_hbm, hin_ref),
-            )
+            ((sh_hbm, sh_ref), (fr_hbm, fr_ref), (f_hbm, f_ref), (hin_hbm, hin_ref))
         )
     ]
-    for c in loads:
+    lo, hi = GROUP_BINS - 128, 2 * GROUP_BINS + 128
+    parts = [
+        pltpu.make_async_copy(
+            x_hbm.at[:, pl.ds(a, b - a)], xp.at[:, pl.ds(128 + a, b - a)], xsem.at[4 + k]
+        )
+        for k, (a, b) in enumerate(((lo, hi), (hi, BINS), (0, lo)))
+    ]
+    for c in small[:2] + parts + small[2:]:
         c.start()
 
     barrier = pltpu.get_barrier_semaphore()
@@ -123,61 +125,60 @@
     def _():
         xp[:, 128 + BINS :] = jnp.zeros((ROWS, 128), F32)
 
-    loads[0].wait()
-    loads[1].wait()
+    small[0].wait()
+    small[1].wait()
     for s in range(SEGS):
         shb[s] = jnp.broadcast_to(sh_ref[:, s : s + 1], (ROWS, 128))
         frb[s] = jnp.broadcast_to(fr_ref[:, s : s + 1], (ROWS, 128))
 
-    with jax.named_scope("xwait"):
-        loads[2].wait()
-
     def piece(i):
         return lax.rem(i + NPZ, NP)
 
+    def own_bins(t):
+        return first_bin(0, t)
+
+    def first_bin(r, t):
+        zq, j = lax.div(t, NPZ), lax.rem(t, NPZ)
+        return pl.multiple_of(zq * GROUP_BINS + lax.rem(y + r, NY) * OWN + j * PW, 128)
+
+    def warp(c):
+        width = CHUNK + 256
+        b = pl.multiple_of(c * CHUNK, 128)
+        v = xp[:, pl.ds(b, width)]
+        seg = lax.div(b, SEG)
+        d = jnp.concatenate([shb[seg]] * (width // 128), axis=1)
+        f = jnp.concatenate([frb[seg]] * (CHUNK // 128), axis=1)
+        v = jnp.where(d < 0, pltpu.roll(v, 4, 1), v)
+        v = jnp.where((d & 2) != 0, pltpu.roll(v, width - 2, 1), v)
+        v = jnp.where((d & 1) != 0, pltpu.roll(v, width - 1, 1), v)
+        lower = v[:, 128 : 128 + CHUNK]
+        upper = pltpu.roll(v, width - 1, 1)[:, 128 : 128 + CHUNK]
+        ws[:, pl.ds(b, CHUNK)] = (1.0 - f) * lower + f * upper
+
+    def warp_group(g):
+        zq = lax.rem(g + 1, NZ)
+
+        def one(k, carry):
+            warp(zq * (GROUP_BINS // CHUNK) + k)
+            return carry
+
+        lax.fori_loop(0, GROUP_BINS // CHUNK, one, 0)
+
     def y_copy(r, t):
-        return rcopy(ws.at[r - 1, t], wg.at[t, y], y_s.at[r - 1], y_r.at[t, r - 1], y_dev(r))
-
-    def warp(i):
-        t = piece(i)
-        zq, j = lax.div(t, NPZ), lax.rem(t, NPZ)
-        for r in range(NY):
-            b = zq * (NY * OWN) + lax.rem(y + r, NY) * OWN + j * PW
-            v = xp[:, pl.ds(pl.multiple_of(b, 128), PW + 256)]
-            s = lax.div(b, SEG)
-            reps = (PW + 256) // 128
-            d = jnp.concatenate([shb[s]] * reps, axis=1)
-            f = jnp.concatenate([frb[s]] * (PW // 128), axis=1)
-            width = PW + 256
-            v = jnp.where(d < 0, pltpu.roll(v, 4, 1), v)
-            v = jnp.where((d & 2) != 0, pltpu.roll(v, width - 2, 1), v)
-            v = jnp.where((d & 1) != 0, pltpu.roll(v, width - 1, 1), v)
-            lower = v[:, 128 : 128 + PW]
-            upper = pltpu.roll(v, width - 1, 1)[:, 128 : 128 + PW]
-            out = (1.0 - f) * lower + f * upper
-            if r == 0:
-                wg[t, y] = out
-            else:
-                ws[r - 1, t] = out
-
-    def send(i):
-        t = piece(i)
-        for r in range(1, NY):
-            y_copy(r, t).start()
-
-    def warp_early(i, carry):
-        warp(i)
-        return carry
-
-    def send_early(i, carry):
-        send(i)
-        return carry
-
+        src = ws.at[:, pl.ds(first_bin(r, t), PW)]
+        return rcopy(src, wg.at[t, NY - r - 1], y_s.at[r - 1], y_r.at[t, NY - r - 1], y_dev(r))
+
+    def send_group(g):
+        zq = lax.rem(g + 1, NZ)
+        for j in range(NPZ):
+            for r in range(1, NY):
+                y_copy(r, zq * NPZ + j).start()
+
+    parts[0].wait()
     with jax.named_scope("warps"):
-        lax.fori_loop(0, FIRST, warp_early, 0)
-    loads[3].wait()
-    loads[4].wait()
-    fbuf[y] = f_ref[...]
+        warp_group(0)
+    small[2].wait()
+    fbuf[0] = f_ref[...]
     with jax.named_scope("barrier"):
         pl.semaphore_wait(
             barrier,
@@ -185,11 +186,14 @@
         )
 
     f_copies = [
-        rcopy(f_ref, fbuf.at[y], f_s.at[r - 1], f_r.at[r - 1], y_dev(r)) for r in range(1, NY)
+        rcopy(f_ref, fbuf.at[NY - r], f_s.at[r - 1], f_r.at[NY - r - 1], y_dev(r)) for r in range(1, NY)
     ]
     for c in f_copies:
         c.start()
-    lax.fori_loop(0, FIRST, send_early, 0)
+    send_group(0)
+    parts[1].wait()
+    parts[2].wait()
+    small[3].wait()
 
     to_right = rcopy(
         xp.at[:, pl.ds(BINS, 128)], xp.at[:, pl.ds(0, 128)], halo_s.at[0], halo_r.at[0], (p, m + 1)
@@ -223,6 +227,14 @@
     def _():
         for j in range(NPZ):
             hc[z * NPZ + j] = hin_ref[:, j * PW : (j + 1) * PW]
+
+    def early(g, carry):
+        warp_group(g)
+        send_group(g)
+        return carry
+
+    with jax.named_scope("warps"):
+        lax.fori_loop(1, EARLY, early, 0)
 
     with jax.named_scope("fwait"):
         for c in f_copies:
@@ -271,20 +283,23 @@
         return rcopy(hbuf.at[t], hbuf.at[t], h_s, h_r.at[t], (outer, m))
 
     def step(i, carry):
-        @pl.when((i >= FIRST - AHEAD) & (i + AHEAD < NP))
+        @pl.when(i == 8)
         def _():
-            @pl.when(i + AHEAD == NP - NPZ - 1)
-            def _():
-                @pl.when(m > 0)
-                def _():
-                    to_right.wait_recv()
-
-                @pl.when(m < 15)
-                def _():
-                    to_left.wait_recv()
-
-            warp(i + AHEAD)
-            send(i + AHEAD)
+            @pl.when(m < 15)
+            def _():
+                to_left.wait_recv()
+
+            warp_group(NZ - 2)
+            send_group(NZ - 2)
+
+        @pl.when(i == 11)
+        def _():
+            @pl.when(m > 0)
+            def _():
+                to_right.wait_recv()
+
+            warp_group(NZ - 1)
+            send_group(NZ - 1)
 
         @pl.when(i < NP)
         def _():
@@ -292,7 +307,8 @@
             with jax.named_scope("ywait"):
                 for r in range(1, NY):
                     y_copy(r, t).wait_recv()
-            w_hi, w_lo = halves(wg[t].reshape(GROUP, PW))
+            mine = ws[:, pl.ds(own_bins(t), PW)]
+            w_hi, w_lo = halves(jnp.concatenate([mine, wg[t].reshape(GROUP - ROWS, PW)], axis=0))
             both = jnp.concatenate([w_hi, w_lo], axis=0)
             wgb[t] = both
             n = jnp.dot(lhs[...], jnp.concatenate([both, w_hi], axis=0), preferred_element_type=F32)
@@ -360,16 +376,15 @@
     base = 2 * GROUP
     gram = both[base : base + RANK] + both[base + RANK : base + 2 * RANK]
     for k in range(NY):
-        t1s[k] = jnp.concatenate(
-            [proj[k * ROWS : (k + 1) * ROWS], gram[0:ROWS], gram[ROWS : 2 * ROWS], jnp.zeros((ROWS, 32), F32)],
-            axis=1,
-        )
+        t1s[k, 0:8] = jnp.concatenate([gram[8 * q : 8 * q + 8] for q in range(4)], axis=1)
+        rows = proj[k * ROWS : (k + 1) * ROWS]
+        t1s[k, 8:12] = jnp.concatenate([rows[4 * q : 4 * q + 4] for q in range(4)], axis=1)
 
     me = y * 8 + ml
 
     def t_copy(k):
         return rcopy(
-            t1s.at[lax.rem(y + lax.div(k, 8), NY)], t1r.at[me], t1_s.at[k], t1_r.at[k], plane_dev(k)
+            t1s.at[lax.div(k, 8)], t1r.at[me], t1_s.at[k], t1_r.at[k], plane_dev(k)
         )
 
     def t_start(k, carry):
@@ -385,7 +400,7 @@
         return carry
 
     lax.fori_loop(1, PEERS, t_start, 0)
-    t1r[me] = t1s[y]
+    t1r[me] = t1s[0]
     with jax.named_scope("t1wait"):
         lax.fori_loop(1, PEERS, t_recv, 0)
     part = t1r[0]
@@ -397,10 +412,11 @@
     with jax.named_scope("t3wait"):
         t3_copy.wait_recv()
     total = part + t3r[...]
-    gram_sum = jnp.concatenate([total[:, 32:64], total[:, 64:96]], axis=0)
+    gram_sum = jnp.concatenate([total[0:8, 32 * q : 32 * q + 32] for q in range(4)], axis=0)
+    proj_sum = jnp.concatenate([total[8:12, 32 * q : 32 * q + 32] for q in range(4)], axis=0)
     f = f_ref[...]
     bottom = jnp.dot(f, gram_sum, precision=exact_mode, preferred_element_type=F32) + EPSILON
-    w_ref[...] = f * total[:, 0:32] / bottom
+    w_ref[...] = f * proj_sum / bottom
 
     for c in f_copies + [t3_copy]:
         c.wait_send()
@@ -428,7 +444,7 @@
         hc_sent(NPZ)
 
     for r in range(1, NY):
-        rcopy(ws.at[r - 1], ws.at[r - 1], y_s.at[r - 1], y_s.at[r - 1], y_dev(r)).wait_send()
+        rcopy(wg.at[:, r - 1], wg.at[:, r - 1], y_s.at[r - 1], y_s.at[r - 1], y_dev(r)).wait_send()
     rcopy(cout, cout, c_s, c_s, (inner, m)).wait_send()
 
     @pl.when(has_outer)
@@ -455,8 +471,8 @@
             pltpu.VMEM((ROWS, BINS + 256), F32),
             pltpu.VMEM((SEGS, ROWS, 128), jnp.int32),
             pltpu.VMEM((SEGS, ROWS, 128), F32),
-            pltpu.VMEM((NY - 1, NP, ROWS, PW), F32),
-            pltpu.VMEM((NP, NY, ROWS, PW), F32),
+            pltpu.VMEM((ROWS, BINS), F32),
+            pltpu.VMEM((NP, NY - 1, ROWS, PW), F32),
             pltpu.VMEM((NP, 2 * GROUP, PW), BF16),
             pltpu.VMEM((2, NP, RANK, PW), F32),
             pltpu.VMEM((NP, RANK, PW), F32),
@@ -468,11 +484,11 @@
             pltpu.VMEM((RANK, RANK), F32),
             pltpu.VMEM((NZ + 2, RANK, RANK), F32),
             pltpu.VMEM((2 * GROUP + 2 * RANK, 2 * RANK), F32),
-            pltpu.VMEM((NY, ROWS, 128), F32),
-            pltpu.VMEM((PEERS, ROWS, 128), F32),
-            pltpu.VMEM((ROWS, 128), F32),
-            pltpu.VMEM((ROWS, 128), F32),
-            dma((5,)),
+            pltpu.VMEM((NY, 12, 128), F32),
+            pltpu.VMEM((PEERS, 12, 128), F32),
+            pltpu.VMEM((12, 128), F32),
+            pltpu.VMEM((12, 128), F32),
+            dma((7,)),
             dma((2,)),
             dma((2,)),
             dma((NY - 1,)),
@@ -493,7 +509,7 @@
             dma(()),
         ],
         compiler_params=pltpu.CompilerParams(
-            collective_id=0, has_side_effects=True, vmem_limit_bytes=48 * 1024 * 1024
+            collective_id=0, has_side_effects=True, vmem_limit_bytes=66_000_000
         ),
     )(spectra, shifts, fractions, pixel_factors, spectral_factors)
 

time: 86.2 us -> 81.4 us (0.944)
  local copies, waits for them, and re-layouts: 5.62 us -> 2.83 us
  Pallas kernels: 79.6 us -> 77.7 us
    unnamed x12 -> x2, local copies, waits for them, and re-layouts: 5.62 us -> 2.83 us
    pallas_call x1, Pallas kernels: 79.6 us -> 77.7 us  [body(): pl.pallas_call(kernel, out_shape=(jax.ShapeDtypeStruct((ROWS, RANK), F32)...]
where the time goes in v3:
time: 81.4 us; the launch traced here: 81.2 us
  Pallas kernels  77.7 us (95%)
  local copies, waits for them, and re-layouts  2.83 us (3%)
    pallas_call x1, Pallas kernels, body(): pl.pallas_call(kernel, out_shape=(jax.ShapeDtypeStruct((ROWS, RANK), F32)...  77.7 us
    unnamed x2, local copies, waits for them, and re-layouts  2.83 us

profile of v3, /device:TPU:1, one launch (start us, length us, event | category | flops | bytes accessed | tf_op | source)
XLA Modules:
  0.0 81.2 jit_solution(1761036294663872105)
XLA Ops:
  0.6 77.7 %shard_map.68 = (f32[16,32]{1,0:T(8,128)}, f32[32,768]{1,0:T(8,128)}) custom-call(f32[16,24576]{1,0:T(8,128)} %x_hbm.1, s32[16,12]{1,0:T(8,128)} %sh_hbm.1, f32[16,12]{1,0:T(8,128)} %fr_hbm.1, f32[16,32]{1,0:T(8,128)} %f_hbm.1, f32[32,768]{1,0:T(8,128)} %hin_hbm.1), custom_call_target="tpu_custom_call" | custom-call | tf_op jit(solution)/shard_map/pallas_call | solution.py:458
  78.4 1.3 %copy.9 = f32[16,32]{1,0:T(8,128)} copy(f32[16,32]{1,0:T(8,128)} %get-tuple-element.4) | data formatting | bytes 4096
  79.7 1.5 %copy.10 = f32[32,768]{1,0:T(8,128)} copy(f32[32,768]{1,0:T(8,128)} %get-tuple-element.5) | data formatting | bytes 196608

commit v4 on v3

--- a/solution.py
+++ b/solution.py
@@ -17,7 +17,10 @@
 NPZ = OWN // PW
 NP = NZ * NPZ
 GROUP = NY * ROWS
-LAGS = (5, 13, 21, 24)
+LAGS = (7, 16, 24, 24)
+SUB = 2
+SUB_ROWS = RANK // SUB
+DIRECT = 2
 CHUNK = 1024
 GROUP_BINS = NY * OWN
 EARLY = 6
@@ -38,9 +41,9 @@
     x_hbm, sh_hbm, fr_hbm, f_hbm, hin_hbm, w_ref, hout_ref,
     sh_ref, fr_ref, f_ref, hin_ref,
     xp, shb, frb, ws, wg, wgb, cbuf, cout, hbuf, hc, rbuf, fbuf, lhs, gsend, gbuf, acc,
-    t1s, t1r, t3s, t3r,
+    grams, t1s, t1r, t3s, t3r, row_s, row_r,
     xsem, halo_s, halo_r, f_s, f_r, hc_s, hc_r, g_s, g_r,
-    y_s, y_r, c_s, c_r, h_s, h_r, t1_s, t1_r, t3_s, t3_r,
+    y_s, y_r, c_s, c_r, h_s, h_r, t1_s, t1_r, t3_s, t3_r, r_s, r_r,
 ):
     p, m = lax.axis_index("pix"), lax.axis_index("mz")
     z, y = lax.div(p, NY), lax.rem(p, NY)
@@ -98,14 +101,12 @@
 
     for k in range(1, PEERS):
         greet(plane_dev(k))
-    half = lax.div(z, NZ // 2) * (NZ // 2)
-    for r in range(1, NZ // 2):
-        greet(((half + lax.rem(z + r, NZ // 2)) * NY + y, m))
-    greet(far)
-
-    @pl.when(center)
-    def _():
-        greet((inner, m))
+    def line_dev(k):
+        other = lax.rem(mh + lax.div(k, NZ), 2)
+        return (lax.rem(z + k, NZ) * NY + y, other * 8 + ml)
+
+    for k in range(1, 2 * NZ):
+        greet(line_dev(k))
 
     @pl.when(m == 7)
     def _():
@@ -144,25 +145,34 @@
     def warp(c):
         width = CHUNK + 256
         b = pl.multiple_of(c * CHUNK, 128)
+        seg = lax.div(b, SEG)
+        d, f = shb[seg], frb[seg]
+
+        def wide(v, lanes):
+            return jnp.concatenate([v] * (lanes // 128), axis=1)
+
         v = xp[:, pl.ds(b, width)]
-        seg = lax.div(b, SEG)
-        d = jnp.concatenate([shb[seg]] * (width // 128), axis=1)
-        f = jnp.concatenate([frb[seg]] * (CHUNK // 128), axis=1)
-        v = jnp.where(d < 0, pltpu.roll(v, 4, 1), v)
-        v = jnp.where((d & 2) != 0, pltpu.roll(v, width - 2, 1), v)
-        v = jnp.where((d & 1) != 0, pltpu.roll(v, width - 1, 1), v)
-        lower = v[:, 128 : 128 + CHUNK]
-        upper = pltpu.roll(v, width - 1, 1)[:, 128 : 128 + CHUNK]
-        ws[:, pl.ds(b, CHUNK)] = (1.0 - f) * lower + f * upper
+        v = jnp.where(wide(d, width) < 0, pltpu.roll(v, 4, 1), v)
+        shifted = [v] + [pltpu.roll(v, width - k, 1) for k in range(1, 5)]
+        shifted = [u[:, 128 : 128 + CHUNK] for u in shifted]
+        rest = wide(d & 3, CHUNK)
+        high, odd = rest >= 2, (rest & 1) != 0
+
+        def pick(k):
+            return jnp.where(
+                high,
+                jnp.where(odd, shifted[k + 3], shifted[k + 2]),
+                jnp.where(odd, shifted[k + 1], shifted[k]),
+            )
+
+        f = wide(f, CHUNK)
+        ws[:, pl.ds(b, CHUNK)] = (1.0 - f) * pick(0) + f * pick(1)
 
     def warp_group(g):
         zq = lax.rem(g + 1, NZ)
 
-        def one(k, carry):
+        for k in range(GROUP_BINS // CHUNK):
             warp(zq * (GROUP_BINS // CHUNK) + k)
-            return carry
-
-        lax.fori_loop(0, GROUP_BINS // CHUNK, one, 0)
 
     def y_copy(r, t):
         src = ws.at[:, pl.ds(first_bin(r, t), PW)]
@@ -182,7 +192,7 @@
     with jax.named_scope("barrier"):
         pl.semaphore_wait(
             barrier,
-            PEERS + NZ // 2 - 1 + jnp.where(center, 1, 0) + jnp.where((m == 7) | (m == 8), 1, 0),
+            PEERS - 1 + 2 * NZ - 1 + jnp.where((m == 7) | (m == 8), 1, 0),
         )
 
     f_copies = [
@@ -273,14 +283,17 @@
         g_other.wait_recv()
         gbuf[NZ + 1] = total + gbuf[NZ]
 
-    def c_copy(t):
-        return rcopy(cout.at[t], cbuf.at[slot, t], c_s, c_r.at[slot, t], (inner, m))
-
-    def c_wait(s, t):
-        rcopy(cout.at[t], cbuf.at[s, t], c_s, c_r.at[s, t], (inner, m)).wait_recv()
-
-    def h_copy(t):
-        return rcopy(hbuf.at[t], hbuf.at[t], h_s, h_r.at[t], (outer, m))
+    def rows_of(q):
+        return pl.ds(q * SUB_ROWS, SUB_ROWS)
+
+    def c_copy(t, q, s):
+        return rcopy(
+            cout.at[t, rows_of(q)], cbuf.at[s, t, rows_of(q)], c_s, c_r.at[s, t, q], (inner, m)
+        )
+
+    def h_copy(t, q, dev):
+        part = hbuf.at[t, rows_of(q)]
+        return rcopy(part, part, h_s, h_r.at[t, q], dev)
 
     def step(i, carry):
         @pl.when(i == 8)
@@ -315,15 +328,18 @@
 
             @pl.when(has_outer)
             def _():
-                with jax.named_scope("cwait"):
-                    c_wait(0, t)
-                cout[t] = n + cbuf[0, t]
+                for q in range(SUB):
+                    with jax.named_scope("cwait"):
+                        c_copy(t, q, 0).wait_recv()
+                    part = n[q * SUB_ROWS : (q + 1) * SUB_ROWS]
+                    cout[t, rows_of(q)] = part + cbuf[0, t, rows_of(q)]
+                    c_copy(t, q, slot).start()
 
             @pl.when(jnp.logical_not(has_outer))
             def _():
                 cout[t] = n
-
-            c_copy(t).start()
+                for q in range(SUB):
+                    c_copy(t, q, slot).start()
 
             @pl.when(center)
             def _():
@@ -344,18 +360,27 @@
 
             @pl.when(center)
             def _():
-                with jax.named_scope("xcwait"):
-                    c_wait(1, t)
-                hbuf[t] = rbuf[t] * (cout[t] + cbuf[1, t])
+                for q in range(SUB):
+                    with jax.named_scope("xcwait"):
+                        c_copy(t, q, 1).wait_recv()
+                    r = rows_of(q)
+                    hbuf[t, r] = rbuf[t, r] * (cout[t, r] + cbuf[1, t, r])
+                    h_copy(t, q, (outer, m)).start()
+
+                    @pl.when(k >= NP - DIRECT)
+                    def _():
+                        for far_out in (2, 3):
+                            h_copy(t, q, (outward(far_out) * NY + y, m)).start()
 
             @pl.when(jnp.logical_not(center))
             def _():
-                with jax.named_scope("hwait"):
-                    h_copy(t).wait_recv()
-
-            @pl.when(has_outer)
-            def _():
-                h_copy(t).start()
+                for q in range(SUB):
+                    with jax.named_scope("hwait"):
+                        h_copy(t, q, (outer, m)).wait_recv()
+
+                    @pl.when(has_outer & (k < NP - DIRECT))
+                    def _():
+                        h_copy(t, q, (outer, m)).start()
 
             h = hbuf[t]
             h_hi, h_lo = halves(h)
@@ -375,10 +400,12 @@
     proj = both[0:GROUP] + both[GROUP : 2 * GROUP]
     base = 2 * GROUP
     gram = both[base : base + RANK] + both[base + RANK : base + 2 * RANK]
+    grams[...] = jnp.concatenate([gram[8 * q : 8 * q + 8] for q in range(4)], axis=1)
+    my_gram = grams[pl.ds(z, 1)]
     for k in range(NY):
-        t1s[k, 0:8] = jnp.concatenate([gram[8 * q : 8 * q + 8] for q in range(4)], axis=1)
         rows = proj[k * ROWS : (k + 1) * ROWS]
-        t1s[k, 8:12] = jnp.concatenate([rows[4 * q : 4 * q + 4] for q in range(4)], axis=1)
+        t1s[k, 0:4] = jnp.concatenate([rows[4 * q : 4 * q + 4] for q in range(4)], axis=1)
+        t1s[k, 4:5] = my_gram
 
     me = y * 8 + ml
 
@@ -406,14 +433,36 @@
     part = t1r[0]
     for k in range(1, PEERS):
         part = part + t1r[k]
-    t3s[...] = part
+    t3s[...] = part[0:4]
+    row_s[...] = part[4:5]
     t3_copy = rcopy(t3s, t3r, t3_s, t3_r, far)
     t3_copy.start()
+    here = mh * NZ + z
+
+    def row_copy(k):
+        return rcopy(row_s, row_r.at[here], r_s.at[k], r_r.at[k], line_dev(k))
+
+    def row_start(k, carry):
+        row_copy(k).start()
+        return carry
+
+    def row_recv(k, carry):
+        row_copy(k).wait_recv()
+        return carry
+
+    def row_sent(k, carry):
+        row_copy(k).wait_send()
+        return carry
+
+    lax.fori_loop(1, 2 * NZ, row_start, 0)
+    row_r[here] = part[4:5]
     with jax.named_scope("t3wait"):
         t3_copy.wait_recv()
-    total = part + t3r[...]
-    gram_sum = jnp.concatenate([total[0:8, 32 * q : 32 * q + 32] for q in range(4)], axis=0)
-    proj_sum = jnp.concatenate([total[8:12, 32 * q : 32 * q + 32] for q in range(4)], axis=0)
+        lax.fori_loop(1, 2 * NZ, row_recv, 0)
+    proj4 = part[0:4] + t3r[...]
+    gram8 = jnp.concatenate([row_r[k] + row_r[NZ + k] for k in range(NZ)], axis=0)
+    gram_sum = jnp.concatenate([gram8[:, 32 * q : 32 * q + 32] for q in range(4)], axis=0)
+    proj_sum = jnp.concatenate([proj4[:, 32 * q : 32 * q + 32] for q in range(4)], axis=0)
     f = f_ref[...]
     bottom = jnp.dot(f, gram_sum, precision=exact_mode, preferred_element_type=F32) + EPSILON
     w_ref[...] = f * proj_sum / bottom
@@ -421,6 +470,7 @@
     for c in f_copies + [t3_copy]:
         c.wait_send()
     lax.fori_loop(1, PEERS, t_sent, 0)
+    lax.fori_loop(1, 2 * NZ, row_sent, 0)
 
     @pl.when(m < 15)
     def _():
@@ -447,9 +497,18 @@
         rcopy(wg.at[:, r - 1], wg.at[:, r - 1], y_s.at[r - 1], y_s.at[r - 1], y_dev(r)).wait_send()
     rcopy(cout, cout, c_s, c_s, (inner, m)).wait_send()
 
-    @pl.when(has_outer)
-    def _():
-        rcopy(hbuf, hbuf, h_s, h_s, (outer, m)).wait_send()
+    def h_sent(pieces):
+        part = hbuf.at[pl.ds(0, pieces)]
+        rcopy(part, part, h_s, h_s, (outer, m)).wait_send()
+
+    @pl.when(center)
+    def _():
+        h_sent(NP)
+        h_sent(2 * DIRECT)
+
+    @pl.when(has_outer & jnp.logical_not(center))
+    def _():
+        h_sent(NP - DIRECT)
 
 
 def body(spectra, shifts, fractions, pixel_factors, spectral_factors):
@@ -484,10 +543,13 @@
             pltpu.VMEM((RANK, RANK), F32),
             pltpu.VMEM((NZ + 2, RANK, RANK), F32),
             pltpu.VMEM((2 * GROUP + 2 * RANK, 2 * RANK), F32),
-            pltpu.VMEM((NY, 12, 128), F32),
-            pltpu.VMEM((PEERS, 12, 128), F32),
-            pltpu.VMEM((12, 128), F32),
-            pltpu.VMEM((12, 128), F32),
+            pltpu.VMEM((NZ, 128), F32),
+            pltpu.VMEM((NY, 5, 128), F32),
+            pltpu.VMEM((PEERS, 5, 128), F32),
+            pltpu.VMEM((4, 128), F32),
+            pltpu.VMEM((4, 128), F32),
+            pltpu.VMEM((1, 128), F32),
+            pltpu.VMEM((2 * NZ, 1, 128), F32),
             dma((7,)),
             dma((2,)),
             dma((2,)),
@@ -500,13 +562,15 @@
             dma((NY - 1,)),
             dma((NP, NY - 1)),
             dma(()),
-            dma((2, NP)),
+            dma((2, NP, SUB)),
             dma(()),
-            dma((NP,)),
+            dma((NP, SUB)),
             dma((PEERS,)),
             dma((PEERS,)),
             dma(()),
             dma(()),
+            dma((2 * NZ,)),
+            dma((2 * NZ,)),
         ],
         compiler_params=pltpu.CompilerParams(
             collective_id=0, has_side_effects=True, vmem_limit_bytes=66_000_000

time: 81.4 us -> 82.7 us (1.016)
  Pallas kernels: 77.7 us -> 79 us
    pallas_call x1, Pallas kernels: 77.7 us -> 79 us  [body(): pl.pallas_call(kernel, out_shape=(jax.ShapeDtypeStruct((ROWS, RANK), F32)...]
where the time goes in v4:
time: 82.7 us; the launch traced here: 82.4 us
  Pallas kernels  79 us (96%)
  local copies, waits for them, and re-layouts  2.83 us (3%)
    pallas_call x1, Pallas kernels, body(): pl.pallas_call(kernel, out_shape=(jax.ShapeDtypeStruct((ROWS, RANK), F32)...  79 us
    unnamed x2, local copies, waits for them, and re-layouts  2.83 us

profile of v4, /device:TPU:1, one launch (start us, length us, event | category | flops | bytes accessed | tf_op | source)
XLA Modules:
  0.0 82.4 jit_solution(9200051499327298816)
XLA Ops:
  0.6 79.0 %shard_map.68 = (f32[16,32]{1,0:T(8,128)}, f32[32,768]{1,0:T(8,128)}) custom-call(f32[16,24576]{1,0:T(8,128)} %x_hbm.1, s32[16,12]{1,0:T(8,128)} %sh_hbm.1, f32[16,12]{1,0:T(8,128)} %fr_hbm.1, f32[16,32]{1,0:T(8,128)} %f_hbm.1, f32[32,768]{1,0:T(8,128)} %hin_hbm.1), custom_call_target="tpu_custom_call" | custom-call | tf_op jit(solution)/shard_map/pallas_call | solution.py:517
  79.6 1.3 %copy.9 = f32[16,32]{1,0:T(8,128)} copy(f32[16,32]{1,0:T(8,128)} %get-tuple-element.4) | data formatting | bytes 4096
  80.9 1.5 %copy.10 = f32[32,768]{1,0:T(8,128)} copy(f32[32,768]{1,0:T(8,128)} %get-tuple-element.5) | data formatting | bytes 196608

commit v5 on v4

--- a/solution.py
+++ b/solution.py
@@ -17,14 +17,14 @@
 NPZ = OWN // PW
 NP = NZ * NPZ
 GROUP = NY * ROWS
-LAGS = (7, 16, 24, 24)
+LAGS = (5, 12, 20, 24)
 SUB = 2
 SUB_ROWS = RANK // SUB
 DIRECT = 2
 CHUNK = 1024
 GROUP_BINS = NY * OWN
 EARLY = 6
-PEERS = 32
+CHIPS = 16
 MESH = pl.DeviceIdType.MESH
 F32 = jnp.float32
 BF16 = jnp.bfloat16
@@ -41,9 +41,9 @@
     x_hbm, sh_hbm, fr_hbm, f_hbm, hin_hbm, w_ref, hout_ref,
     sh_ref, fr_ref, f_ref, hin_ref,
     xp, shb, frb, ws, wg, wgb, cbuf, cout, hbuf, hc, rbuf, fbuf, lhs, gsend, gbuf, acc,
-    grams, t1s, t1r, t3s, t3r, row_s, row_r,
+    f_all, t0s, t0r, t1s, t1r, t3s, t3r,
     xsem, halo_s, halo_r, f_s, f_r, hc_s, hc_r, g_s, g_r,
-    y_s, y_r, c_s, c_r, h_s, h_r, t1_s, t1_r, t3_s, t3_r, r_s, r_r,
+    y_s, y_r, c_s, c_r, h_s, h_r, t0_s, t0_r, t1_s, t1_r, t3_s, t3_r,
 ):
     p, m = lax.axis_index("pix"), lax.axis_index("mz")
     z, y = lax.div(p, NY), lax.rem(p, NY)
@@ -93,28 +93,34 @@
     def greet(dev):
         pl.semaphore_signal(barrier, inc=1, device_id=dev, device_id_type=MESH)
 
+    core = lax.rem(ml, 2)
+    partner = (p, m + 1 - 2 * core)
+
     def plane_dev(k):
         return (
-            z * NY + lax.rem(y + lax.div(k, 8), NY),
-            mh * 8 + lax.rem(ml + lax.rem(k, 8), 8),
+            z * NY + lax.rem(y + lax.div(k, 4), NY),
+            mh * 8 + lax.rem(ml + 2 * lax.rem(k, 4), 8),
         )
 
-    for k in range(1, PEERS):
+    for k in range(1, CHIPS):
         greet(plane_dev(k))
-    def line_dev(k):
-        other = lax.rem(mh + lax.div(k, NZ), 2)
-        return (lax.rem(z + k, NZ) * NY + y, other * 8 + ml)
-
-    for k in range(1, 2 * NZ):
-        greet(line_dev(k))
-
-    @pl.when(m == 7)
-    def _():
-        greet((p, 8))
-
-    @pl.when(m == 8)
-    def _():
-        greet((p, 7))
+    greet(partner)
+    greet(far)
+    half = lax.div(z, NZ // 2) * (NZ // 2)
+    for r in range(1, NZ // 2):
+        greet(((half + lax.rem(z + r, NZ // 2)) * NY + y, m))
+
+    @pl.when(center)
+    def _():
+        greet((inner, m))
+
+    @pl.when((core == 0) & (m > 0))
+    def _():
+        greet((p, m - 1))
+
+    @pl.when((core == 1) & (m < 15))
+    def _():
+        greet((p, m + 1))
 
     acc[...] = jnp.zeros_like(acc)
 
@@ -188,15 +194,15 @@
     with jax.named_scope("warps"):
         warp_group(0)
     small[2].wait()
-    fbuf[0] = f_ref[...]
+    f_all[...] = jnp.concatenate([f_ref[...], jnp.zeros((ROWS, 128 - RANK), F32)], axis=1)
     with jax.named_scope("barrier"):
         pl.semaphore_wait(
             barrier,
-            PEERS - 1 + 2 * NZ - 1 + jnp.where((m == 7) | (m == 8), 1, 0),
+            CHIPS + 1 + NZ // 2 - 1 + jnp.where(center, 1, 0) + jnp.where((m == 0) | (m == 15), 0, 1),
         )
 
     f_copies = [
-        rcopy(f_ref, fbuf.at[NY - r], f_s.at[r - 1], f_r.at[NY - r - 1], y_dev(r)) for r in range(1, NY)
+        rcopy(f_all, fbuf.at[NY - r - 1], f_s.at[r - 1], f_r.at[NY - r - 1], y_dev(r)) for r in range(1, NY)
     ]
     for c in f_copies:
         c.start()
@@ -249,7 +255,7 @@
     with jax.named_scope("fwait"):
         for c in f_copies:
             c.wait_recv()
-    fg = fbuf[...].reshape(GROUP, RANK)
+    fg = jnp.concatenate([f_all[...], fbuf[...].reshape(GROUP - ROWS, 128)], axis=0)[:, 0:RANK]
     gy = lax.dot_general(fg, fg, (((0,), (0,)), ((), ())), precision=exact_mode, preferred_element_type=F32)
     f_hi, f_lo = halves(fg.T)
     lhs[...] = jnp.concatenate([f_hi, f_hi, f_lo], axis=1)
@@ -400,77 +406,52 @@
     proj = both[0:GROUP] + both[GROUP : 2 * GROUP]
     base = 2 * GROUP
     gram = both[base : base + RANK] + both[base + RANK : base + 2 * RANK]
-    grams[...] = jnp.concatenate([gram[8 * q : 8 * q + 8] for q in range(4)], axis=1)
-    my_gram = grams[pl.ds(z, 1)]
+    gram8 = jnp.concatenate([gram[8 * q : 8 * q + 8] for q in range(4)], axis=1)
     for k in range(NY):
         rows = proj[k * ROWS : (k + 1) * ROWS]
-        t1s[k, 0:4] = jnp.concatenate([rows[4 * q : 4 * q + 4] for q in range(4)], axis=1)
-        t1s[k, 4:5] = my_gram
-
-    me = y * 8 + ml
+        t0s[k, 0:8] = gram8
+        t0s[k, 8:12] = jnp.concatenate([rows[4 * q : 4 * q + 4] for q in range(4)], axis=1)
+    t0_copy = rcopy(t0s, t0r, t0_s, t0_r, partner)
+    t0_copy.start()
+    with jax.named_scope("t0wait"):
+        t0_copy.wait_recv()
+    t1s[...] = t0s[...] + t0r[...]
+
+    me = y * 4 + lax.div(ml, 2)
 
     def t_copy(k):
-        return rcopy(
-            t1s.at[lax.div(k, 8)], t1r.at[me], t1_s.at[k], t1_r.at[k], plane_dev(k)
-        )
-
-    def t_start(k, carry):
-        t_copy(k).start()
-        return carry
-
-    def t_recv(k, carry):
-        t_copy(k).wait_recv()
-        return carry
-
-    def t_sent(k, carry):
-        t_copy(k).wait_send()
-        return carry
-
-    lax.fori_loop(1, PEERS, t_start, 0)
+        return rcopy(t1s.at[lax.div(k, 4)], t1r.at[me], t1_s.at[k], t1_r.at[k], plane_dev(k))
+
+    t1_copies = [t_copy(k) for k in range(1, CHIPS)]
+    for c in t1_copies:
+        c.start()
     t1r[me] = t1s[0]
     with jax.named_scope("t1wait"):
-        lax.fori_loop(1, PEERS, t_recv, 0)
-    part = t1r[0]
-    for k in range(1, PEERS):
-        part = part + t1r[k]
-    t3s[...] = part[0:4]
-    row_s[...] = part[4:5]
+        for c in t1_copies:
+            c.wait_recv()
+    sums = [t1r[k] for k in range(CHIPS)]
+    while len(sums) > 1:
+        sums = [a + b for a, b in zip(sums[::2], sums[1::2])]
+    t3s[...] = sums[0]
     t3_copy = rcopy(t3s, t3r, t3_s, t3_r, far)
     t3_copy.start()
-    here = mh * NZ + z
-
-    def row_copy(k):
-        return rcopy(row_s, row_r.at[here], r_s.at[k], r_r.at[k], line_dev(k))
-
-    def row_start(k, carry):
-        row_copy(k).start()
-        return carry
-
-    def row_recv(k, carry):
-        row_copy(k).wait_recv()
-        return carry
-
-    def row_sent(k, carry):
-        row_copy(k).wait_send()
-        return carry
-
-    lax.fori_loop(1, 2 * NZ, row_start, 0)
-    row_r[here] = part[4:5]
     with jax.named_scope("t3wait"):
         t3_copy.wait_recv()
-        lax.fori_loop(1, 2 * NZ, row_recv, 0)
-    proj4 = part[0:4] + t3r[...]
-    gram8 = jnp.concatenate([row_r[k] + row_r[NZ + k] for k in range(NZ)], axis=0)
-    gram_sum = jnp.concatenate([gram8[:, 32 * q : 32 * q + 32] for q in range(4)], axis=0)
-    proj_sum = jnp.concatenate([proj4[:, 32 * q : 32 * q + 32] for q in range(4)], axis=0)
+    total = sums[0] + t3r[...]
+    gram_sum = jnp.concatenate([total[0:8, 32 * q : 32 * q + 32] for q in range(4)], axis=0)
+    proj_sum = jnp.concatenate([total[8:12, 32 * q : 32 * q + 32] for q in range(4)], axis=0)
     f = f_ref[...]
-    bottom = jnp.dot(f, gram_sum, precision=exact_mode, preferred_element_type=F32) + EPSILON
+    g_hi, g_lo = halves(gram_sum)
+    own_hi, own_lo = halves(f)
+    bottom = EPSILON + jnp.dot(
+        jnp.concatenate([own_hi, own_hi, own_lo], axis=1),
+        jnp.concatenate([g_hi, g_lo, g_hi], axis=0),
+        preferred_element_type=F32,
+    )
     w_ref[...] = f * proj_sum / bottom
 
-    for c in f_copies + [t3_copy]:
+    for c in f_copies + t1_copies + [t0_copy, t3_copy]:
         c.wait_send()
-    lax.fori_loop(1, PEERS, t_sent, 0)
-    lax.fori_loop(1, 2 * NZ, row_sent, 0)
 
     @pl.when(m < 15)
     def _():
@@ -538,18 +519,18 @@
             pltpu.VMEM((NP, RANK, PW), F32),
             pltpu.VMEM((NP, RANK, PW), F32),
             pltpu.VMEM((NP, RANK, PW), F32),
-            pltpu.VMEM((NY, ROWS, RANK), F32),
+            pltpu.VMEM((NY - 1, ROWS, 128), F32),
             pltpu.VMEM((RANK, 3 * GROUP), BF16),
             pltpu.VMEM((RANK, RANK), F32),
             pltpu.VMEM((NZ + 2, RANK, RANK), F32),
             pltpu.VMEM((2 * GROUP + 2 * RANK, 2 * RANK), F32),
-            pltpu.VMEM((NZ, 128), F32),
-            pltpu.VMEM((NY, 5, 128), F32),
-            pltpu.VMEM((PEERS, 5, 128), F32),
-            pltpu.VMEM((4, 128), F32),
-            pltpu.VMEM((4, 128), F32),
-            pltpu.VMEM((1, 128), F32),
-            pltpu.VMEM((2 * NZ, 1, 128), F32),
+            pltpu.VMEM((ROWS, 128), F32),
+            pltpu.VMEM((NY, 12, 128), F32),
+            pltpu.VMEM((NY, 12, 128), F32),
+            pltpu.VMEM((NY, 12, 128), F32),
+            pltpu.VMEM((CHIPS, 12, 128), F32),
+            pltpu.VMEM((12, 128), F32),
+            pltpu.VMEM((12, 128), F32),
             dma((7,)),
             dma((2,)),
             dma((2,)),
@@ -565,12 +546,12 @@
             dma((2, NP, SUB)),
             dma(()),
             dma((NP, SUB)),
-            dma((PEERS,)),
-            dma((PEERS,)),
-            dma(()),
-            dma(()),
-            dma((2 * NZ,)),
-            dma((2 * NZ,)),
+            dma(()),
+            dma(()),
+            dma((CHIPS,)),
+            dma((CHIPS,)),
+            dma(()),
+            dma(()),
         ],
         compiler_params=pltpu.CompilerParams(
             collective_id=0, has_side_effects=True, vmem_limit_bytes=66_000_000

time: 82.7 us -> 79.5 us (0.961)
  Pallas kernels: 79 us -> 75.8 us
    pallas_call x1, Pallas kernels: 79 us -> 75.8 us  [body(): pl.pallas_call(kernel, out_shape=(jax.ShapeDtypeStruct((ROWS, RANK), F32)...]
where the time goes in v5:
time: 79.5 us; the launch traced here: 79.3 us
  Pallas kernels  75.8 us (95%)
  local copies, waits for them, and re-layouts  2.83 us (4%)
    pallas_call x1, Pallas kernels, body(): pl.pallas_call(kernel, out_shape=(jax.ShapeDtypeStruct((ROWS, RANK), F32)...  75.8 us
    unnamed x2, local copies, waits for them, and re-layouts  2.83 us

profile of v5, /device:TPU:1, one launch (start us, length us, event | category | flops | bytes accessed | tf_op | source)
XLA Modules:
  0.0 79.3 jit_solution(263676802847669515)
XLA Ops:
  0.6 75.8 %shard_map.68 = (f32[16,32]{1,0:T(8,128)}, f32[32,768]{1,0:T(8,128)}) custom-call(f32[16,24576]{1,0:T(8,128)} %x_hbm.1, s32[16,12]{1,0:T(8,128)} %sh_hbm.1, f32[16,12]{1,0:T(8,128)} %fr_hbm.1, f32[16,32]{1,0:T(8,128)} %f_hbm.1, f32[32,768]{1,0:T(8,128)} %hin_hbm.1), custom_call_target="tpu_custom_call" | custom-call | tf_op jit(solution)/shard_map/pallas_call | solution.py:498
  76.5 1.3 %copy.9 = f32[16,32]{1,0:T(8,128)} copy(f32[16,32]{1,0:T(8,128)} %get-tuple-element.4) | data formatting | bytes 4096
  77.8 1.5 %copy.10 = f32[32,768]{1,0:T(8,128)} copy(f32[32,768]{1,0:T(8,128)} %get-tuple-element.5) | data formatting | bytes 196608

commit v6 on v5

--- a/solution.py
+++ b/solution.py
@@ -17,7 +17,8 @@
 NPZ = OWN // PW
 NP = NZ * NPZ
 GROUP = NY * ROWS
-LAGS = (5, 12, 20, 24)
+LAGS = (4, 13, 22, 24)
+LATE_WARP = 6
 SUB = 2
 SUB_ROWS = RANK // SUB
 DIRECT = 2
@@ -302,24 +303,6 @@
         return rcopy(part, part, h_s, h_r.at[t, q], dev)
 
     def step(i, carry):
-        @pl.when(i == 8)
-        def _():
-            @pl.when(m < 15)
-            def _():
-                to_left.wait_recv()
-
-            warp_group(NZ - 2)
-            send_group(NZ - 2)
-
-        @pl.when(i == 11)
-        def _():
-            @pl.when(m > 0)
-            def _():
-                to_right.wait_recv()
-
-            warp_group(NZ - 1)
-            send_group(NZ - 1)
-
         @pl.when(i < NP)
         def _():
             t = piece(i)
@@ -331,6 +314,23 @@
             both = jnp.concatenate([w_hi, w_lo], axis=0)
             wgb[t] = both
             n = jnp.dot(lhs[...], jnp.concatenate([both, w_hi], axis=0), preferred_element_type=F32)
+
+            @pl.when(i == jnp.where(has_outer, 0, LATE_WARP))
+            def _():
+                @pl.when(m < 15)
+                def _():
+                    to_left.wait_recv()
+
+                @pl.when(m > 0)
+                def _():
+                    to_right.wait_recv()
+
+                def late(g, carry):
+                    warp_group(g)
+                    send_group(g)
+                    return carry
+
+                lax.fori_loop(EARLY, NZ, late, 0)
 
             @pl.when(has_outer)
             def _():
@@ -498,8 +498,8 @@
     return pl.pallas_call(
         kernel,
         out_shape=(
-            jax.ShapeDtypeStruct((ROWS, RANK), F32),
-            jax.ShapeDtypeStruct((RANK, OWN), F32),
+            pltpu.VMEM((ROWS, RANK), F32),
+            pltpu.VMEM((RANK, OWN), F32),
         ),
         in_specs=[pl.BlockSpec(memory_space=pltpu.HBM)] * 5,
         out_specs=(vmem, vmem),

time: 79.5 us -> 77.2 us (0.971)
  local copies, waits for them, and re-layouts: 2.83 us -> 1.24 us
    unnamed x2, local copies, waits for them, and re-layouts: 2.83 us -> 1.24 us
where the time goes in v6:
time: 77.2 us; the launch traced here: 77 us
  Pallas kernels  75.1 us (97%)
  local copies, waits for them, and re-layouts  1.24 us (2%)
    pallas_call x1, Pallas kernels, body(): pl.pallas_call(kernel, out_shape=(pltpu.VMEM((ROWS, RANK), F32), pltpu.VM...  75.1 us

profile of v6, /device:TPU:1, one launch (start us, length us, event | category | flops | bytes accessed | tf_op | source)
XLA Modules:
  0.0 77.0 jit_solution(10187929392319967883)
XLA Ops:
  0.6 75.1 %shard_map.68 = (f32[16,32]{1,0:T(8,128)S(1)}, f32[32,768]{1,0:T(8,128)S(1)}) custom-call(f32[16,24576]{1,0:T(8,128)} %x_hbm.1, s32[16,12]{1,0:T(8,128)} %sh_hbm.1, f32[16,12]{1,0:T(8,128)} %fr_hbm.1, f32[16,32]{1,0:T(8,128)} %f_hbm.1, f32[32,768]{1,0:T(8,128)} %hin_hbm.1), custom_call_target="tpu_custom_call" | custom-call | tf_op jit(solution)/shard_map/pallas_call | solution.py:498
  75.8 0.6 copy.9
  76.4 0.6 copy.10

commit v7 on v6

--- a/solution.py
+++ b/solution.py
@@ -17,8 +17,8 @@
 NPZ = OWN // PW
 NP = NZ * NPZ
 GROUP = NY * ROWS
-LAGS = (4, 13, 22, 24)
-LATE_WARP = 6
+LAGS = (6, 14, 22, 24)
+LATE_OUT, LATE_FAR = 6, 8
 SUB = 2
 SUB_ROWS = RANK // SUB
 DIRECT = 2
@@ -44,7 +44,7 @@
     xp, shb, frb, ws, wg, wgb, cbuf, cout, hbuf, hc, rbuf, fbuf, lhs, gsend, gbuf, acc,
     f_all, t0s, t0r, t1s, t1r, t3s, t3r,
     xsem, halo_s, halo_r, f_s, f_r, hc_s, hc_r, g_s, g_r,
-    y_s, y_r, c_s, c_r, h_s, h_r, t0_s, t0_r, t1_s, t1_r, t3_s, t3_r,
+    y_s, y_r, c_s, c_r, h_s, x_r, t0_s, t0_r, t1_s, t1_r, t3_s, t3_r,
 ):
     p, m = lax.axis_index("pix"), lax.axis_index("mz")
     z, y = lax.div(p, NY), lax.rem(p, NY)
@@ -54,7 +54,6 @@
     outer = jnp.where(low_side, p - NY, p + NY)
     depth = jnp.where(low_side, NZ // 2 - 1 - z, z - NZ // 2)
     center = depth == 0
-    slot = jnp.where(center, 1, 0)
     has_outer = depth < NZ // 2 - 1
     lag = jnp.where(
         depth == 0, LAGS[0], jnp.where(depth == 1, LAGS[1], jnp.where(depth == 2, LAGS[2], LAGS[3]))
@@ -183,7 +182,7 @@
 
     def y_copy(r, t):
         src = ws.at[:, pl.ds(first_bin(r, t), PW)]
-        return rcopy(src, wg.at[t, NY - r - 1], y_s.at[r - 1], y_r.at[t, NY - r - 1], y_dev(r))
+        return rcopy(src, wg.at[t, NY - r - 1], y_s.at[r - 1], y_r.at[t], y_dev(r))
 
     def send_group(g):
         zq = lax.rem(g + 1, NZ)
@@ -203,7 +202,7 @@
         )
 
     f_copies = [
-        rcopy(f_all, fbuf.at[NY - r - 1], f_s.at[r - 1], f_r.at[NY - r - 1], y_dev(r)) for r in range(1, NY)
+        rcopy(f_all, fbuf.at[NY - r - 1], f_s, f_r, y_dev(r)) for r in range(1, NY)
     ]
     for c in f_copies:
         c.start()
@@ -229,21 +228,16 @@
 
     near = jnp.where(low_side, NZ // 2 - 1, NZ // 2)
 
-    def h_part(j):
-        t = z * NPZ + j
-        dev = (jnp.where(center, inner, near * NY + y), m)
-        return rcopy(hin_ref.at[:, pl.ds(j * PW, PW)], hc.at[t], hc_s, hc_r.at[t], dev)
-
-    def h_relay(t):
-        return rcopy(hc.at[t], hc.at[t], hc_s, hc_r.at[t], (inner, m))
-
-    for j in range(NPZ):
-        h_part(j).start()
+    h_part = rcopy(hin_ref, hc.at[z], hc_s, hc_r.at[z], (jnp.where(center, inner, near * NY + y), m))
+
+    def h_relay(zk):
+        return rcopy(hc.at[zk], hc.at[zk], hc_s, hc_r.at[zk], (inner, m))
+
+    h_part.start()
 
     @pl.when(center)
     def _():
-        for j in range(NPZ):
-            hc[z * NPZ + j] = hin_ref[:, j * PW : (j + 1) * PW]
+        hc[z] = hin_ref[...]
 
     def early(g, carry):
         warp_group(g)
@@ -254,19 +248,29 @@
         lax.fori_loop(1, EARLY, early, 0)
 
     with jax.named_scope("fwait"):
-        for c in f_copies:
-            c.wait_recv()
+        rcopy(fbuf, fbuf, f_s, f_r, y_dev(1)).wait_recv()
     fg = jnp.concatenate([f_all[...], fbuf[...].reshape(GROUP - ROWS, 128)], axis=0)[:, 0:RANK]
     gy = lax.dot_general(fg, fg, (((0,), (0,)), ((), ())), precision=exact_mode, preferred_element_type=F32)
     f_hi, f_lo = halves(fg.T)
     lhs[...] = jnp.concatenate([f_hi, f_hi, f_lo], axis=1)
 
-    g_half = rcopy(gsend, gbuf.at[z], g_s, g_r.at[z], (near * NY + y, m))
-    g_other = rcopy(gsend, gbuf.at[NZ], g_s, g_r.at[NZ], (inner, m))
+    g_half = rcopy(gsend, gbuf.at[depth], g_s, g_r.at[depth], (near * NY + y, m))
+    g_other = rcopy(gsend, gbuf.at[0], g_s, g_r.at[0], (inner, m))
 
     def outward(k):
         return jnp.where(low_side, NZ // 2 - 1 - k, NZ // 2 + k)
 
+    def warp_late():
+        @pl.when(m < 15)
+        def _():
+            to_left.wait_recv()
+
+        @pl.when(m > 0)
+        def _():
+            to_right.wait_recv()
+
+        lax.fori_loop(EARLY, NZ, early, 0)
+
     @pl.when(jnp.logical_not(center))
     def _():
         gsend[...] = gy
@@ -276,86 +280,87 @@
     def _():
         total = gy
         for k in range(1, NZ // 2):
-            zk = outward(k)
-            rcopy(gsend, gbuf.at[zk], g_s, g_r.at[zk], (inner, m)).wait_recv()
-            total = total + gbuf[zk]
+            rcopy(gsend, gbuf.at[k], g_s, g_r.at[k], (inner, m)).wait_recv()
+            total = total + gbuf[k]
         gsend[...] = total
         g_other.start()
+        warp_late()
         with jax.named_scope("relay"):
             for k in range(1, NZ // 2):
-                for j in range(NPZ):
-                    t = outward(k) * NPZ + j
-                    h_relay(t).wait_recv()
-                    h_relay(t).start()
+                h_relay(outward(k)).wait_recv()
+                h_relay(outward(k)).start()
         g_other.wait_recv()
-        gbuf[NZ + 1] = total + gbuf[NZ]
+        gbuf[NZ // 2] = total + gbuf[0]
+
+    across = (m == 7) | (m == 8)
+    late_step = jnp.where(has_outer, jnp.where(center, -1, jnp.where(across, LATE_FAR, 0)), LATE_OUT)
 
     def rows_of(q):
         return pl.ds(q * SUB_ROWS, SUB_ROWS)
 
-    def c_copy(t, q, s):
-        return rcopy(
-            cout.at[t, rows_of(q)], cbuf.at[s, t, rows_of(q)], c_s, c_r.at[s, t, q], (inner, m)
-        )
+    def c_copy(t, q):
+        dst = cbuf.at[0, t, rows_of(q)]
+        return rcopy(cout.at[t, rows_of(q)], dst, c_s, c_r.at[t, q], (inner, m))
+
+    def cx_copy(t, q):
+        dst = cbuf.at[1, t, rows_of(q)]
+        return rcopy(cout.at[t, rows_of(q)], dst, c_s, x_r.at[t, q], (inner, m))
+
+    def c_send(t, q):
+        @pl.when(center)
+        def _():
+            cx_copy(t, q).start()
+
+        @pl.when(jnp.logical_not(center))
+        def _():
+            c_copy(t, q).start()
 
     def h_copy(t, q, dev):
         part = hbuf.at[t, rows_of(q)]
-        return rcopy(part, part, h_s, h_r.at[t, q], dev)
+        return rcopy(part, part, h_s, x_r.at[t, q], dev)
 
     def step(i, carry):
         @pl.when(i < NP)
         def _():
             t = piece(i)
             with jax.named_scope("ywait"):
-                for r in range(1, NY):
-                    y_copy(r, t).wait_recv()
+                rcopy(wg.at[t], wg.at[t], y_s.at[0], y_r.at[t], y_dev(1)).wait_recv()
             mine = ws[:, pl.ds(own_bins(t), PW)]
             w_hi, w_lo = halves(jnp.concatenate([mine, wg[t].reshape(GROUP - ROWS, PW)], axis=0))
             both = jnp.concatenate([w_hi, w_lo], axis=0)
             wgb[t] = both
             n = jnp.dot(lhs[...], jnp.concatenate([both, w_hi], axis=0), preferred_element_type=F32)
 
-            @pl.when(i == jnp.where(has_outer, 0, LATE_WARP))
-            def _():
-                @pl.when(m < 15)
-                def _():
-                    to_left.wait_recv()
-
-                @pl.when(m > 0)
-                def _():
-                    to_right.wait_recv()
-
-                def late(g, carry):
-                    warp_group(g)
-                    send_group(g)
-                    return carry
-
-                lax.fori_loop(EARLY, NZ, late, 0)
+            @pl.when(i == late_step)
+            def _():
+                warp_late()
 
             @pl.when(has_outer)
             def _():
                 for q in range(SUB):
                     with jax.named_scope("cwait"):
-                        c_copy(t, q, 0).wait_recv()
+                        c_copy(t, q).wait_recv()
                     part = n[q * SUB_ROWS : (q + 1) * SUB_ROWS]
                     cout[t, rows_of(q)] = part + cbuf[0, t, rows_of(q)]
-                    c_copy(t, q, slot).start()
+                    c_send(t, q)
 
             @pl.when(jnp.logical_not(has_outer))
             def _():
                 cout[t] = n
                 for q in range(SUB):
-                    c_copy(t, q, slot).start()
+                    c_send(t, q)
 
             @pl.when(center)
             def _():
-                @pl.when(lax.div(t, NPZ * (NZ // 2)) != lax.div(z, NZ // 2))
+                zq, j = lax.div(t, NPZ), lax.rem(t, NPZ)
+
+                @pl.when((j == 0) & (lax.div(zq, NZ // 2) != lax.div(z, NZ // 2)))
                 def _():
                     with jax.named_scope("hcwait"):
-                        h_relay(t).wait_recv()
-
-                own = hc[t]
-                bottom = jnp.dot(gbuf[NZ + 1], own, precision=exact_mode, preferred_element_type=F32) + EPSILON
+                        h_relay(zq).wait_recv()
+
+                own = hc[zq, :, pl.ds(pl.multiple_of(j * PW, 128), PW)]
+                bottom = jnp.dot(gbuf[NZ // 2], own, precision=exact_mode, preferred_element_type=F32) + EPSILON
                 rbuf[t] = own / bottom
 
         k = i - lag
@@ -368,7 +373,7 @@
             def _():
                 for q in range(SUB):
                     with jax.named_scope("xcwait"):
-                        c_copy(t, q, 1).wait_recv()
+                        cx_copy(t, q).wait_recv()
                     r = rows_of(q)
                     hbuf[t, r] = rbuf[t, r] * (cout[t, r] + cbuf[1, t, r])
                     h_copy(t, q, (outer, m)).start()
@@ -450,7 +455,8 @@
     )
     w_ref[...] = f * proj_sum / bottom
 
-    for c in f_copies + t1_copies + [t0_copy, t3_copy]:
+    rcopy(fbuf, fbuf, f_s, f_r, y_dev(1)).wait_send()
+    for c in t1_copies + [t0_copy, t3_copy]:
         c.wait_send()
 
     @pl.when(m < 15)
@@ -462,17 +468,12 @@
         to_left.wait_send()
 
     g_half.wait_send()
-    def hc_sent(pieces):
-        part = hc.at[pl.ds(0, pieces)]
+    h_part.wait_send()
+
+    @pl.when(center)
+    def _():
+        part = hc.at[pl.ds(0, NZ // 2 - 1)]
         rcopy(part, part, hc_s, hc_s, (inner, m)).wait_send()
-
-    @pl.when(center)
-    def _():
-        hc_sent(NPZ * (NZ // 2))
-
-    @pl.when(jnp.logical_not(center))
-    def _():
-        hc_sent(NPZ)
 
     for r in range(1, NY):
         rcopy(wg.at[:, r - 1], wg.at[:, r - 1], y_s.at[r - 1], y_s.at[r - 1], y_dev(r)).wait_send()
@@ -517,12 +518,12 @@
             pltpu.VMEM((2, NP, RANK, PW), F32),
             pltpu.VMEM((NP, RANK, PW), F32),
             pltpu.VMEM((NP, RANK, PW), F32),
-            pltpu.VMEM((NP, RANK, PW), F32),
+            pltpu.VMEM((NZ, RANK, OWN), F32),
             pltpu.VMEM((NP, RANK, PW), F32),
             pltpu.VMEM((NY - 1, ROWS, 128), F32),
             pltpu.VMEM((RANK, 3 * GROUP), BF16),
             pltpu.VMEM((RANK, RANK), F32),
-            pltpu.VMEM((NZ + 2, RANK, RANK), F32),
+            pltpu.VMEM((NZ // 2 + 1, RANK, RANK), F32),
             pltpu.VMEM((2 * GROUP + 2 * RANK, 2 * RANK), F32),
             pltpu.VMEM((ROWS, 128), F32),
             pltpu.VMEM((NY, 12, 128), F32),
@@ -534,16 +535,16 @@
             dma((7,)),
             dma((2,)),
             dma((2,)),
+            dma(()),
+            dma(()),
+            dma(()),
+            dma((NZ,)),
+            dma(()),
+            dma((NZ // 2,)),
             dma((NY - 1,)),
-            dma((NY - 1,)),
-            dma(()),
             dma((NP,)),
             dma(()),
-            dma((NZ + 1,)),
-            dma((NY - 1,)),
-            dma((NP, NY - 1)),
-            dma(()),
-            dma((2, NP, SUB)),
+            dma((NP, SUB)),
             dma(()),
             dma((NP, SUB)),
             dma(()),

time: 77.2 us -> 76 us (0.984)
  Pallas kernels: 75.1 us -> 74 us
    pallas_call x1, Pallas kernels: 75.1 us -> 74 us  [body(): pl.pallas_call(kernel, out_shape=(pltpu.VMEM((ROWS, RANK), F32), pltpu.VM...]
where the time goes in v7:
time: 76 us; the launch traced here: 75.9 us
  Pallas kernels  74 us (97%)
  local copies, waits for them, and re-layouts  1.24 us (2%)
    pallas_call x1, Pallas kernels, body(): pl.pallas_call(kernel, out_shape=(pltpu.VMEM((ROWS, RANK), F32), pltpu.VM...  74 us

profile of v7, /device:TPU:1, one launch (start us, length us, event | category | flops | bytes accessed | tf_op | source)
XLA Modules:
  0.0 75.9 jit_solution(6494828818430552263)
XLA Ops:
  0.6 74.0 %shard_map.68 = (f32[16,32]{1,0:T(8,128)S(1)}, f32[32,768]{1,0:T(8,128)S(1)}) custom-call(f32[16,24576]{1,0:T(8,128)} %x_hbm.1, s32[16,12]{1,0:T(8,128)} %sh_hbm.1, f32[16,12]{1,0:T(8,128)} %fr_hbm.1, f32[16,32]{1,0:T(8,128)} %f_hbm.1, f32[32,768]{1,0:T(8,128)} %hin_hbm.1), custom_call_target="tpu_custom_call" | custom-call | tf_op jit(solution)/shard_map/pallas_call | solution.py:499
  74.6 0.6 copy.9
  75.2 0.6 copy.10

commit v8 on v7

--- a/solution.py
+++ b/solution.py
@@ -17,14 +17,15 @@
 NPZ = OWN // PW
 NP = NZ * NPZ
 GROUP = NY * ROWS
-LAGS = (6, 14, 22, 24)
-LATE_OUT, LATE_FAR = 6, 8
+LAGS = (5, 13, 21, 24)
+LATE, LATE_FAR = 3, 7
 SUB = 2
 SUB_ROWS = RANK // SUB
-DIRECT = 2
+DIRECT = 3
 CHUNK = 1024
 GROUP_BINS = NY * OWN
 EARLY = 6
+LATE_CHUNKS = (NZ - EARLY) * (GROUP_BINS // CHUNK)
 CHIPS = 16
 MESH = pl.DeviceIdType.MESH
 F32 = jnp.float32
@@ -41,7 +42,7 @@
 def kernel(
     x_hbm, sh_hbm, fr_hbm, f_hbm, hin_hbm, w_ref, hout_ref,
     sh_ref, fr_ref, f_ref, hin_ref,
-    xp, shb, frb, ws, wg, wgb, cbuf, cout, hbuf, hc, rbuf, fbuf, lhs, gsend, gbuf, acc,
+    xp, shb, frb, ws, wg, wgb, cbuf, cout, hbuf, hc, fbuf, lhs, gsend, gbuf, acc,
     f_all, t0s, t0r, t1s, t1r, t3s, t3r,
     xsem, halo_s, halo_r, f_s, f_r, hc_s, hc_r, g_s, g_r,
     y_s, y_r, c_s, c_r, h_s, x_r, t0_s, t0_r, t1_s, t1_r, t3_s, t3_r,
@@ -78,7 +79,7 @@
             ((sh_hbm, sh_ref), (fr_hbm, fr_ref), (f_hbm, f_ref), (hin_hbm, hin_ref))
         )
     ]
-    lo, hi = GROUP_BINS - 128, 2 * GROUP_BINS + 128
+    lo, hi = 3 * GROUP_BINS - 128, 4 * GROUP_BINS + 128
     parts = [
         pltpu.make_async_copy(
             x_hbm.at[:, pl.ds(a, b - a)], xp.at[:, pl.ds(128 + a, b - a)], xsem.at[4 + k]
@@ -138,8 +139,12 @@
         shb[s] = jnp.broadcast_to(sh_ref[:, s : s + 1], (ROWS, 128))
         frb[s] = jnp.broadcast_to(fr_ref[:, s : s + 1], (ROWS, 128))
 
+    def group_z(g):
+        step = lax.div(g, 2)
+        return jnp.where(lax.rem(g, 2) == 0, NZ // 2 - 1 - step, NZ // 2 + step)
+
     def piece(i):
-        return lax.rem(i + NPZ, NP)
+        return group_z(lax.div(i, NPZ)) * NPZ + lax.rem(i, NPZ)
 
     def own_bins(t):
         return first_bin(0, t)
@@ -175,7 +180,7 @@
         ws[:, pl.ds(b, CHUNK)] = (1.0 - f) * pick(0) + f * pick(1)
 
     def warp_group(g):
-        zq = lax.rem(g + 1, NZ)
+        zq = group_z(g)
 
         for k in range(GROUP_BINS // CHUNK):
             warp(zq * (GROUP_BINS // CHUNK) + k)
@@ -185,7 +190,7 @@
         return rcopy(src, wg.at[t, NY - r - 1], y_s.at[r - 1], y_r.at[t], y_dev(r))
 
     def send_group(g):
-        zq = lax.rem(g + 1, NZ)
+        zq = group_z(g)
         for j in range(NPZ):
             for r in range(1, NY):
                 y_copy(r, zq * NPZ + j).start()
@@ -260,16 +265,23 @@
     def outward(k):
         return jnp.where(low_side, NZ // 2 - 1 - k, NZ // 2 + k)
 
-    def warp_late():
-        @pl.when(m < 15)
+    def warp_late(e):
+        chunks = GROUP_BINS // CHUNK
+        g = EARLY + lax.div(e, chunks)
+
+        @pl.when((e == 0) & (m > 0))
+        def _():
+            to_right.wait_recv()
+
+        @pl.when((e == 2 * chunks - 1) & (m < 15))
         def _():
             to_left.wait_recv()
 
-        @pl.when(m > 0)
-        def _():
-            to_right.wait_recv()
-
-        lax.fori_loop(EARLY, NZ, early, 0)
+        warp(group_z(g) * chunks + lax.rem(e, chunks))
+
+        @pl.when(lax.rem(e, chunks) == chunks - 1)
+        def _():
+            send_group(g)
 
     @pl.when(jnp.logical_not(center))
     def _():
@@ -284,7 +296,11 @@
             total = total + gbuf[k]
         gsend[...] = total
         g_other.start()
-        warp_late()
+        def late(e, carry):
+            warp_late(e)
+            return carry
+
+        lax.fori_loop(0, LATE_CHUNKS, late, 0)
         with jax.named_scope("relay"):
             for k in range(1, NZ // 2):
                 h_relay(outward(k)).wait_recv()
@@ -293,7 +309,7 @@
         gbuf[NZ // 2] = total + gbuf[0]
 
     across = (m == 7) | (m == 8)
-    late_step = jnp.where(has_outer, jnp.where(center, -1, jnp.where(across, LATE_FAR, 0)), LATE_OUT)
+    late_from = jnp.where(center, -LATE_CHUNKS, jnp.where(across, LATE_FAR, LATE))
 
     def rows_of(q):
         return pl.ds(q * SUB_ROWS, SUB_ROWS)
@@ -331,10 +347,6 @@
             wgb[t] = both
             n = jnp.dot(lhs[...], jnp.concatenate([both, w_hi], axis=0), preferred_element_type=F32)
 
-            @pl.when(i == late_step)
-            def _():
-                warp_late()
-
             @pl.when(has_outer)
             def _():
                 for q in range(SUB):
@@ -350,6 +362,18 @@
                 for q in range(SUB):
                     c_send(t, q)
 
+            late = i - late_from
+
+            @pl.when((late >= 0) & (late < LATE_CHUNKS))
+            def _():
+                warp_late(late)
+
+        k = i - lag
+
+        @pl.when((k >= 0) & (k < NP))
+        def _():
+            t = piece(k)
+
             @pl.when(center)
             def _():
                 zq, j = lax.div(t, NPZ), lax.rem(t, NPZ)
@@ -361,27 +385,19 @@
 
                 own = hc[zq, :, pl.ds(pl.multiple_of(j * PW, 128), PW)]
                 bottom = jnp.dot(gbuf[NZ // 2], own, precision=exact_mode, preferred_element_type=F32) + EPSILON
-                rbuf[t] = own / bottom
-
-        k = i - lag
-
-        @pl.when((k >= 0) & (k < NP))
-        def _():
-            t = piece(k)
-
-            @pl.when(center)
-            def _():
+                ratio = own / bottom
                 for q in range(SUB):
                     with jax.named_scope("xcwait"):
                         cx_copy(t, q).wait_recv()
                     r = rows_of(q)
-                    hbuf[t, r] = rbuf[t, r] * (cout[t, r] + cbuf[1, t, r])
-                    h_copy(t, q, (outer, m)).start()
+                    hbuf[t, r] = ratio[q * SUB_ROWS : (q + 1) * SUB_ROWS] * (cout[t, r] + cbuf[1, t, r])
 
                     @pl.when(k >= NP - DIRECT)
                     def _():
-                        for far_out in (2, 3):
+                        for far_out in (3, 2):
                             h_copy(t, q, (outward(far_out) * NY + y, m)).start()
+
+                    h_copy(t, q, (outer, m)).start()
 
             @pl.when(jnp.logical_not(center))
             def _():
@@ -519,7 +535,6 @@
             pltpu.VMEM((NP, RANK, PW), F32),
             pltpu.VMEM((NP, RANK, PW), F32),
             pltpu.VMEM((NZ, RANK, OWN), F32),
-            pltpu.VMEM((NP, RANK, PW), F32),
             pltpu.VMEM((NY - 1, ROWS, 128), F32),
             pltpu.VMEM((RANK, 3 * GROUP), BF16),
             pltpu.VMEM((RANK, RANK), F32),

time: 76 us -> 77 us (1.013)
  Pallas kernels: 74 us -> 75 us
    pallas_call x1, Pallas kernels: 74 us -> 75 us  [body(): pl.pallas_call(kernel, out_shape=(pltpu.VMEM((ROWS, RANK), F32), pltpu.VM...]
where the time goes in v8:
time: 77 us; the launch traced here: 76.9 us
  Pallas kernels  75 us (97%)
  local copies, waits for them, and re-layouts  1.24 us (2%)
    pallas_call x1, Pallas kernels, body(): pl.pallas_call(kernel, out_shape=(pltpu.VMEM((ROWS, RANK), F32), pltpu.VM...  75 us

profile of v8, /device:TPU:1, one launch (start us, length us, event | category | flops | bytes accessed | tf_op | source)
XLA Modules:
  0.0 76.9 jit_solution(8225752526635394164)
XLA Ops:
  0.6 75.0 %shard_map.68 = (f32[16,32]{1,0:T(8,128)S(1)}, f32[32,768]{1,0:T(8,128)S(1)}) custom-call(f32[16,24576]{1,0:T(8,128)} %x_hbm.1, s32[16,12]{1,0:T(8,128)} %sh_hbm.1, f32[16,12]{1,0:T(8,128)} %fr_hbm.1, f32[16,32]{1,0:T(8,128)} %f_hbm.1, f32[32,768]{1,0:T(8,128)} %hin_hbm.1), custom_call_target="tpu_custom_call" | custom-call | tf_op jit(solution)/shard_map/pallas_call | solution.py:515
  75.6 0.6 copy.9
  76.3 0.6 copy.10

commit v9 on v8

--- a/solution.py
+++ b/solution.py
@@ -21,7 +21,7 @@
 LATE, LATE_FAR = 3, 7
 SUB = 2
 SUB_ROWS = RANK // SUB
-DIRECT = 3
+DIRECT = 2
 CHUNK = 1024
 GROUP_BINS = NY * OWN
 EARLY = 6
@@ -238,7 +238,9 @@
     def h_relay(zk):
         return rcopy(hc.at[zk], hc.at[zk], hc_s, hc_r.at[zk], (inner, m))
 
-    h_part.start()
+    @pl.when(depth <= 1)
+    def _():
+        h_part.start()
 
     @pl.when(center)
     def _():
@@ -250,7 +252,17 @@
         return carry
 
     with jax.named_scope("warps"):
-        lax.fori_loop(1, EARLY, early, 0)
+        lax.fori_loop(1, EARLY // 2, early, 0)
+
+        @pl.when(depth == 2)
+        def _():
+            h_part.start()
+
+        lax.fori_loop(EARLY // 2, EARLY, early, 0)
+
+        @pl.when(depth == 3)
+        def _():
+            h_part.start()
 
     with jax.named_scope("fwait"):
         rcopy(fbuf, fbuf, f_s, f_r, y_dev(1)).wait_recv()
@@ -288,25 +300,29 @@
         gsend[...] = gy
         g_half.start()
 
+    def relay(k):
+        h_relay(outward(k)).wait_recv()
+        h_relay(outward(k)).start()
+
     @pl.when(center)
     def _():
-        total = gy
-        for k in range(1, NZ // 2):
-            rcopy(gsend, gbuf.at[k], g_s, g_r.at[k], (inner, m)).wait_recv()
-            total = total + gbuf[k]
-        gsend[...] = total
-        g_other.start()
+        with jax.named_scope("relay"):
+            relay(1)
+            relay(2)
+            total = gy
+            for k in range(1, NZ // 2):
+                rcopy(gsend, gbuf.at[k], g_s, g_r.at[k], (inner, m)).wait_recv()
+                total = total + gbuf[k]
+            gsend[...] = total
+            gbuf[NZ // 2] = total
+            g_other.start()
+            relay(3)
+
         def late(e, carry):
             warp_late(e)
             return carry
 
         lax.fori_loop(0, LATE_CHUNKS, late, 0)
-        with jax.named_scope("relay"):
-            for k in range(1, NZ // 2):
-                h_relay(outward(k)).wait_recv()
-                h_relay(outward(k)).start()
-        g_other.wait_recv()
-        gbuf[NZ // 2] = total + gbuf[0]
 
     across = (m == 7) | (m == 8)
     late_from = jnp.where(center, -LATE_CHUNKS, jnp.where(across, LATE_FAR, LATE))
@@ -377,6 +393,11 @@
             @pl.when(center)
             def _():
                 zq, j = lax.div(t, NPZ), lax.rem(t, NPZ)
+
+                @pl.when(k == 0)
+                def _():
+                    g_other.wait_recv()
+                    gbuf[NZ // 2] = gbuf[NZ // 2] + gbuf[0]
 
                 @pl.when((j == 0) & (lax.div(zq, NZ // 2) != lax.div(z, NZ // 2)))
                 def _():

time: 77 us -> 74.9 us (0.973)
  Pallas kernels: 75 us -> 72.8 us
    pallas_call x1, Pallas kernels: 75 us -> 72.8 us  [body(): pl.pallas_call(kernel, out_shape=(pltpu.VMEM((ROWS, RANK), F32), pltpu.VM...]
where the time goes in v9:
time: 74.9 us; the launch traced here: 74.7 us
  Pallas kernels  72.8 us (97%)
  local copies, waits for them, and re-layouts  1.24 us (2%)
    pallas_call x1, Pallas kernels, body(): pl.pallas_call(kernel, out_shape=(pltpu.VMEM((ROWS, RANK), F32), pltpu.VM...  72.8 us

profile of v9, /device:TPU:1, one launch (start us, length us, event | category | flops | bytes accessed | tf_op | source)
XLA Modules:
  0.0 74.7 jit_solution(4766934908693444219)
XLA Ops:
  0.6 72.8 %shard_map.68 = (f32[16,32]{1,0:T(8,128)S(1)}, f32[32,768]{1,0:T(8,128)S(1)}) custom-call(f32[16,24576]{1,0:T(8,128)} %x_hbm.1, s32[16,12]{1,0:T(8,128)} %sh_hbm.1, f32[16,12]{1,0:T(8,128)} %fr_hbm.1, f32[16,32]{1,0:T(8,128)} %f_hbm.1, f32[32,768]{1,0:T(8,128)} %hin_hbm.1), custom_call_target="tpu_custom_call" | custom-call | tf_op jit(solution)/shard_map/pallas_call | solution.py:536
  73.5 0.6 copy.9
  74.1 0.6 copy.10

commit v10 on v9

--- a/solution.py
+++ b/solution.py
@@ -18,7 +18,9 @@
 NP = NZ * NPZ
 GROUP = NY * ROWS
 LAGS = (5, 13, 21, 24)
-LATE, LATE_FAR = 3, 7
+LATE = 3
+LATE_FAR = (1, 4, 7, 10)
+SEND_FAR = (-1, 0, 1, 5)
 SUB = 2
 SUB_ROWS = RANK // SUB
 DIRECT = 2
@@ -46,6 +48,7 @@
     f_all, t0s, t0r, t1s, t1r, t3s, t3r,
     xsem, halo_s, halo_r, f_s, f_r, hc_s, hc_r, g_s, g_r,
     y_s, y_r, c_s, c_r, h_s, x_r, t0_s, t0_r, t1_s, t1_r, t3_s, t3_r,
+    seen, seen_edge, told, told_edge,
 ):
     p, m = lax.axis_index("pix"), lax.axis_index("mz")
     z, y = lax.div(p, NY), lax.rem(p, NY)
@@ -56,9 +59,17 @@
     depth = jnp.where(low_side, NZ // 2 - 1 - z, z - NZ // 2)
     center = depth == 0
     has_outer = depth < NZ // 2 - 1
-    lag = jnp.where(
-        depth == 0, LAGS[0], jnp.where(depth == 1, LAGS[1], jnp.where(depth == 2, LAGS[2], LAGS[3]))
-    )
+
+    def by_depth(values):
+        a, b, c, d = values
+        return jnp.where(depth == 0, a, jnp.where(depth == 1, b, jnp.where(depth == 2, c, d)))
+
+    lag = by_depth(LAGS)
+    seam = ((mh == 0) & (z == NZ - 1)) | ((mh == 1) & (z == 0))
+    across = (m == 7) | (m == 8)
+    seam_pix = jnp.where(mh == 0, y, (NZ - 1) * NY + y)
+    seam_dev = (seam_pix, lax.rem(m + 8, 16))
+    seam_edge = (seam_pix, jnp.where(mh == 0, 8, 7))
 
     def y_dev(r):
         return (z * NY + lax.rem(y + r, NY), m)
@@ -106,22 +117,28 @@
     for k in range(1, CHIPS):
         greet(plane_dev(k))
     greet(partner)
-    greet(far)
-    half = lax.div(z, NZ // 2) * (NZ // 2)
-    for r in range(1, NZ // 2):
-        greet(((half + lax.rem(z + r, NZ // 2)) * NY + y, m))
-
-    @pl.when(center)
-    def _():
-        greet((inner, m))
-
-    @pl.when((core == 0) & (m > 0))
+
+    def column_dev(k):
+        return (lax.rem(z + k, NZ) * NY + y, m)
+
+    for k in range(1, NZ):
+        greet(column_dev(k))
+
+    @pl.when((core == 0) & (ml > 0))
     def _():
         greet((p, m - 1))
 
-    @pl.when((core == 1) & (m < 15))
+    @pl.when((core == 1) & (ml < 7))
     def _():
         greet((p, m + 1))
+
+    @pl.when(seam)
+    def _():
+        greet(seam_dev)
+
+    @pl.when(seam & across)
+    def _():
+        greet(seam_edge)
 
     acc[...] = jnp.zeros_like(acc)
 
@@ -203,8 +220,24 @@
     with jax.named_scope("barrier"):
         pl.semaphore_wait(
             barrier,
-            CHIPS + 1 + NZ // 2 - 1 + jnp.where(center, 1, 0) + jnp.where((m == 0) | (m == 15), 0, 1),
+            CHIPS
+            + NZ
+            - 1
+            + jnp.where((ml == 0) | (ml == 7), 0, 1)
+            + jnp.where(seam, 1, 0)
+            + jnp.where(seam & across, 1, 0),
         )
+
+    def signal(sem, dev):
+        pl.semaphore_signal(sem, inc=1, device_id=dev, device_id_type=MESH)
+
+    @pl.when(seam)
+    def _():
+        signal(seen, seam_dev)
+
+    @pl.when(seam & across)
+    def _():
+        signal(seen_edge, seam_edge)
 
     f_copies = [
         rcopy(f_all, fbuf.at[NY - r - 1], f_s, f_r, y_dev(r)) for r in range(1, NY)
@@ -223,13 +256,22 @@
         xp.at[:, pl.ds(128, 128)], xp.at[:, pl.ds(128 + BINS, 128)], halo_s.at[1], halo_r.at[1], (p, m - 1)
     )
 
-    @pl.when(m < 15)
+    @pl.when((m < 15) & (m != 7))
     def _():
         to_right.start()
 
-    @pl.when(m > 0)
+    @pl.when((m > 0) & (m != 8))
     def _():
         to_left.start()
+
+    def send_far():
+        @pl.when(m == 7)
+        def _():
+            to_right.start()
+
+        @pl.when(m == 8)
+        def _():
+            to_left.start()
 
     near = jnp.where(low_side, NZ // 2 - 1, NZ // 2)
 
@@ -249,23 +291,36 @@
     def early(g, carry):
         warp_group(g)
         send_group(g)
+
+        @pl.when(((g == 1) & (depth == 2)) | ((g == 2) & (depth == 3)))
+        def _():
+            h_part.start()
+
         return carry
 
     with jax.named_scope("warps"):
-        lax.fori_loop(1, EARLY // 2, early, 0)
-
-        @pl.when(depth == 2)
-        def _():
-            h_part.start()
-
-        lax.fori_loop(EARLY // 2, EARLY, early, 0)
-
-        @pl.when(depth == 3)
-        def _():
-            h_part.start()
+        lax.fori_loop(1, EARLY, early, 0)
 
     with jax.named_scope("fwait"):
         rcopy(fbuf, fbuf, f_s, f_r, y_dev(1)).wait_recv()
+
+    @pl.when(seam)
+    def _():
+        pl.semaphore_wait(seen, 1)
+        for k in range(1, NZ):
+            signal(told, column_dev(k))
+
+    @pl.when(seam & across)
+    def _():
+        pl.semaphore_wait(seen_edge, 1)
+        send_far()
+        for k in range(1, NZ):
+            signal(told_edge, column_dev(k))
+
+    def send_far_told():
+        pl.semaphore_wait(told_edge, 1)
+        send_far()
+
     fg = jnp.concatenate([f_all[...], fbuf[...].reshape(GROUP - ROWS, 128)], axis=0)[:, 0:RANK]
     gy = lax.dot_general(fg, fg, (((0,), (0,)), ((), ())), precision=exact_mode, preferred_element_type=F32)
     f_hi, f_lo = halves(fg.T)
@@ -322,10 +377,16 @@
             warp_late(e)
             return carry
 
-        lax.fori_loop(0, LATE_CHUNKS, late, 0)
-
-    across = (m == 7) | (m == 8)
-    late_from = jnp.where(center, -LATE_CHUNKS, jnp.where(across, LATE_FAR, LATE))
+        @pl.when(across)
+        def _():
+            send_far_told()
+
+        @pl.when(jnp.logical_not(across))
+        def _():
+            lax.fori_loop(0, LATE_CHUNKS, late, 0)
+
+    late_from = jnp.where(across, by_depth(LATE_FAR), jnp.where(center, -LATE_CHUNKS, LATE))
+    send_far_step = jnp.where(across & jnp.logical_not(seam), by_depth(SEND_FAR), -1)
 
     def rows_of(q):
         return pl.ds(q * SUB_ROWS, SUB_ROWS)
@@ -362,6 +423,10 @@
             both = jnp.concatenate([w_hi, w_lo], axis=0)
             wgb[t] = both
             n = jnp.dot(lhs[...], jnp.concatenate([both, w_hi], axis=0), preferred_element_type=F32)
+
+            @pl.when(i == send_far_step)
+            def _():
+                send_far_told()
 
             @pl.when(has_outer)
             def _():
@@ -475,6 +540,10 @@
     while len(sums) > 1:
         sums = [a + b for a, b in zip(sums[::2], sums[1::2])]
     t3s[...] = sums[0]
+    @pl.when(jnp.logical_not(seam))
+    def _():
+        pl.semaphore_wait(told, 1)
+
     t3_copy = rcopy(t3s, t3r, t3_s, t3_r, far)
     t3_copy.start()
     with jax.named_scope("t3wait"):
@@ -589,6 +658,10 @@
             dma((CHIPS,)),
             dma(()),
             dma(()),
+            pltpu.SemaphoreType.REGULAR,
+            pltpu.SemaphoreType.REGULAR,
+            pltpu.SemaphoreType.REGULAR,
+            pltpu.SemaphoreType.REGULAR,
         ],
         compiler_params=pltpu.CompilerParams(
             collective_id=0, has_side_effects=True, vmem_limit_bytes=66_000_000

time: 74.9 us -> 74.9 us (level)
  no operation moved by 1% of the time
where the time goes in v10:
time: 74.9 us; the launch traced here: 74.7 us
  Pallas kernels  72.9 us (97%)
  local copies, waits for them, and re-layouts  1.24 us (2%)
    pallas_call x1, Pallas kernels, body(): pl.pallas_call(kernel, out_shape=(pltpu.VMEM((ROWS, RANK), F32), pltpu.VM...  72.9 us

profile of v10, /device:TPU:1, one launch (start us, length us, event | category | flops | bytes accessed | tf_op | source)
XLA Modules:
  0.0 74.7 jit_solution(16534070629360052108)
XLA Ops:
  0.6 72.9 %shard_map.68 = (f32[16,32]{1,0:T(8,128)S(1)}, f32[32,768]{1,0:T(8,128)S(1)}) custom-call(f32[16,24576]{1,0:T(8,128)} %x_hbm.1, s32[16,12]{1,0:T(8,128)} %sh_hbm.1, f32[16,12]{1,0:T(8,128)} %fr_hbm.1, f32[16,32]{1,0:T(8,128)} %f_hbm.1, f32[32,768]{1,0:T(8,128)} %hin_hbm.1), custom_call_target="tpu_custom_call" | custom-call | tf_op jit(solution)/shard_map/pallas_call | solution.py:605
  73.5 0.6 copy.9
  74.1 0.6 copy.10

commit v11 on v10

--- a/solution.py
+++ b/solution.py
@@ -18,9 +18,9 @@
 NP = NZ * NPZ
 GROUP = NY * ROWS
 LAGS = (5, 13, 21, 24)
-LATE = 3
-LATE_FAR = (1, 4, 7, 10)
-SEND_FAR = (-1, 0, 1, 5)
+LATE = 2
+LATE_FAR = (2, 7, 11, 16)
+SEND_FAR = (-1, 0, 1, 6)
 SUB = 2
 SUB_ROWS = RANK // SUB
 DIRECT = 2
@@ -158,7 +158,8 @@
 
     def group_z(g):
         step = lax.div(g, 2)
-        return jnp.where(lax.rem(g, 2) == 0, NZ // 2 - 1 - step, NZ // 2 + step)
+        flip = jnp.where((m == 8) & (g >= EARLY), 1, 0)
+        return jnp.where(lax.rem(g, 2) == flip, NZ // 2 - 1 - step, NZ // 2 + step)
 
     def piece(i):
         return group_z(lax.div(i, NPZ)) * NPZ + lax.rem(i, NPZ)
@@ -335,16 +336,18 @@
     def warp_late(e):
         chunks = GROUP_BINS // CHUNK
         g = EARLY + lax.div(e, chunks)
-
-        @pl.when((e == 0) & (m > 0))
+        k = lax.rem(e, chunks)
+        left, right = jnp.where(m == 8, LATE_CHUNKS - 1, 0), jnp.where(m == 8, 0, LATE_CHUNKS - 1)
+
+        @pl.when((e == left) & (m > 0))
         def _():
             to_right.wait_recv()
 
-        @pl.when((e == 2 * chunks - 1) & (m < 15))
+        @pl.when((e == right) & (m < 15))
         def _():
             to_left.wait_recv()
 
-        warp(group_z(g) * chunks + lax.rem(e, chunks))
+        warp(group_z(g) * chunks + jnp.where(m == 8, chunks - 1 - k, k))
 
         @pl.when(lax.rem(e, chunks) == chunks - 1)
         def _():
@@ -381,11 +384,15 @@
         def _():
             send_far_told()
 
+        lax.fori_loop(0, LATE_CHUNKS - 1, late, 0)
+
         @pl.when(jnp.logical_not(across))
         def _():
-            lax.fori_loop(0, LATE_CHUNKS, late, 0)
-
-    late_from = jnp.where(across, by_depth(LATE_FAR), jnp.where(center, -LATE_CHUNKS, LATE))
+            warp_late(LATE_CHUNKS - 1)
+
+    late_from = jnp.where(center, -LATE_CHUNKS, LATE)
+    late_far = jnp.where(across, by_depth(LATE_FAR), -1)
+    late_near = LATE_CHUNKS - jnp.where(across, 1, 0)
     send_far_step = jnp.where(across & jnp.logical_not(seam), by_depth(SEND_FAR), -1)
 
     def rows_of(q):
@@ -445,9 +452,9 @@
 
             late = i - late_from
 
-            @pl.when((late >= 0) & (late < LATE_CHUNKS))
+            @pl.when(((late >= 0) & (late < late_near)) | (i == late_far))
             def _():
-                warp_late(late)
+                warp_late(jnp.where(i == late_far, LATE_CHUNKS - 1, late))
 
         k = i - lag
 

time: 74.9 us -> 74.9 us (level)
  no operation moved by 1% of the time
where the time goes in v11:
time: 74.9 us; the launch traced here: 74.8 us
  Pallas kernels  72.9 us (97%)
  local copies, waits for them, and re-layouts  1.24 us (2%)
    pallas_call x1, Pallas kernels, body(): pl.pallas_call(kernel, out_shape=(pltpu.VMEM((ROWS, RANK), F32), pltpu.VM...  72.9 us

profile of v11, /device:TPU:1, one launch (start us, length us, event | category | flops | bytes accessed | tf_op | source)
XLA Modules:
  0.0 74.8 jit_solution(2878933602293981762)
XLA Ops:
  0.6 72.9 %shard_map.68 = (f32[16,32]{1,0:T(8,128)S(1)}, f32[32,768]{1,0:T(8,128)S(1)}) custom-call(f32[16,24576]{1,0:T(8,128)} %x_hbm.1, s32[16,12]{1,0:T(8,128)} %sh_hbm.1, f32[16,12]{1,0:T(8,128)} %fr_hbm.1, f32[16,32]{1,0:T(8,128)} %f_hbm.1, f32[32,768]{1,0:T(8,128)} %hin_hbm.1), custom_call_target="tpu_custom_call" | custom-call | tf_op jit(solution)/shard_map/pallas_call | solution.py:612
  73.5 0.6 copy.9
  74.1 0.6 copy.10

commit v12 on v11

--- a/solution.py
+++ b/solution.py
@@ -19,8 +19,8 @@
 GROUP = NY * ROWS
 LAGS = (5, 13, 21, 24)
 LATE = 2
-LATE_FAR = (2, 7, 11, 16)
-SEND_FAR = (-1, 0, 1, 6)
+LATE_FAR = (5, 8, 12, 17)
+SEND_FAR = (-1, 0, 0, 2)
 SUB = 2
 SUB_ROWS = RANK // SUB
 DIRECT = 2
@@ -274,43 +274,6 @@
         def _():
             to_left.start()
 
-    near = jnp.where(low_side, NZ // 2 - 1, NZ // 2)
-
-    h_part = rcopy(hin_ref, hc.at[z], hc_s, hc_r.at[z], (jnp.where(center, inner, near * NY + y), m))
-
-    def h_relay(zk):
-        return rcopy(hc.at[zk], hc.at[zk], hc_s, hc_r.at[zk], (inner, m))
-
-    @pl.when(depth <= 1)
-    def _():
-        h_part.start()
-
-    @pl.when(center)
-    def _():
-        hc[z] = hin_ref[...]
-
-    def early(g, carry):
-        warp_group(g)
-        send_group(g)
-
-        @pl.when(((g == 1) & (depth == 2)) | ((g == 2) & (depth == 3)))
-        def _():
-            h_part.start()
-
-        return carry
-
-    with jax.named_scope("warps"):
-        lax.fori_loop(1, EARLY, early, 0)
-
-    with jax.named_scope("fwait"):
-        rcopy(fbuf, fbuf, f_s, f_r, y_dev(1)).wait_recv()
-
-    @pl.when(seam)
-    def _():
-        pl.semaphore_wait(seen, 1)
-        for k in range(1, NZ):
-            signal(told, column_dev(k))
-
     @pl.when(seam & across)
     def _():
         pl.semaphore_wait(seen_edge, 1)
@@ -321,6 +284,43 @@
     def send_far_told():
         pl.semaphore_wait(told_edge, 1)
         send_far()
+
+    near = jnp.where(low_side, NZ // 2 - 1, NZ // 2)
+
+    h_part = rcopy(hin_ref, hc.at[z], hc_s, hc_r.at[z], (jnp.where(center, inner, near * NY + y), m))
+
+    def h_relay(zk):
+        return rcopy(hc.at[zk], hc.at[zk], hc_s, hc_r.at[zk], (inner, m))
+
+    @pl.when(depth <= 1)
+    def _():
+        h_part.start()
+
+    @pl.when(center)
+    def _():
+        hc[z] = hin_ref[...]
+
+    def early(g, carry):
+        warp_group(g)
+        send_group(g)
+
+        @pl.when(((g == 1) & (depth == 2)) | ((g == 2) & (depth == 3)))
+        def _():
+            h_part.start()
+
+        return carry
+
+    with jax.named_scope("warps"):
+        lax.fori_loop(1, EARLY, early, 0)
+
+    with jax.named_scope("fwait"):
+        rcopy(fbuf, fbuf, f_s, f_r, y_dev(1)).wait_recv()
+
+    @pl.when(seam)
+    def _():
+        pl.semaphore_wait(seen, 1)
+        for k in range(1, NZ):
+            signal(told, column_dev(k))
 
     fg = jnp.concatenate([f_all[...], fbuf[...].reshape(GROUP - ROWS, 128)], axis=0)[:, 0:RANK]
     gy = lax.dot_general(fg, fg, (((0,), (0,)), ((), ())), precision=exact_mode, preferred_element_type=F32)
@@ -364,6 +364,10 @@
 
     @pl.when(center)
     def _():
+        @pl.when(across)
+        def _():
+            send_far_told()
+
         with jax.named_scope("relay"):
             relay(1)
             relay(2)
@@ -379,10 +383,6 @@
         def late(e, carry):
             warp_late(e)
             return carry
-
-        @pl.when(across)
-        def _():
-            send_far_told()
 
         lax.fori_loop(0, LATE_CHUNKS - 1, late, 0)
 

time: 74.9 us -> 74.9 us (level)
  no operation moved by 1% of the time
where the time goes in v12:
time: 74.9 us; the launch traced here: 74.8 us
  Pallas kernels  72.9 us (97%)
  local copies, waits for them, and re-layouts  1.24 us (2%)
    pallas_call x1, Pallas kernels, body(): pl.pallas_call(kernel, out_shape=(pltpu.VMEM((ROWS, RANK), F32), pltpu.VM...  72.9 us

profile of v12, /device:TPU:1, one launch (start us, length us, event | category | flops | bytes accessed | tf_op | source)
XLA Modules:
  0.0 74.8 jit_solution(2774797281586947660)
XLA Ops:
  0.6 72.9 %shard_map.68 = (f32[16,32]{1,0:T(8,128)S(1)}, f32[32,768]{1,0:T(8,128)S(1)}) custom-call(f32[16,24576]{1,0:T(8,128)} %x_hbm.1, s32[16,12]{1,0:T(8,128)} %sh_hbm.1, f32[16,12]{1,0:T(8,128)} %fr_hbm.1, f32[16,32]{1,0:T(8,128)} %f_hbm.1, f32[32,768]{1,0:T(8,128)} %hin_hbm.1), custom_call_target="tpu_custom_call" | custom-call | tf_op jit(solution)/shard_map/pallas_call | solution.py:612
  73.5 0.6 copy.9
  74.1 0.6 copy.10

commit v13 on v11

--- a/solution.py
+++ b/solution.py
@@ -19,8 +19,8 @@
 GROUP = NY * ROWS
 LAGS = (5, 13, 21, 24)
 LATE = 2
-LATE_FAR = (2, 7, 11, 16)
-SEND_FAR = (-1, 0, 1, 6)
+LATE_FAR = (8, 12, 16, 20)
+SEND_FAR = (-1, 0, 2, 6)
 SUB = 2
 SUB_ROWS = RANK // SUB
 DIRECT = 2

time: 74.9 us -> 74.9 us (level)
  no operation moved by 1% of the time
where the time goes in v13:
time: 74.9 us; the launch traced here: 74.8 us
  Pallas kernels  72.9 us (97%)
  local copies, waits for them, and re-layouts  1.24 us (2%)
    pallas_call x1, Pallas kernels, body(): pl.pallas_call(kernel, out_shape=(pltpu.VMEM((ROWS, RANK), F32), pltpu.VM...  72.9 us

profile of v13, /device:TPU:1, one launch (start us, length us, event | category | flops | bytes accessed | tf_op | source)
XLA Modules:
  0.0 74.8 jit_solution(3604447853494049710)
XLA Ops:
  0.6 72.9 %shard_map.68 = (f32[16,32]{1,0:T(8,128)S(1)}, f32[32,768]{1,0:T(8,128)S(1)}) custom-call(f32[16,24576]{1,0:T(8,128)} %x_hbm.1, s32[16,12]{1,0:T(8,128)} %sh_hbm.1, f32[16,12]{1,0:T(8,128)} %fr_hbm.1, f32[16,32]{1,0:T(8,128)} %f_hbm.1, f32[32,768]{1,0:T(8,128)} %hin_hbm.1), custom_call_target="tpu_custom_call" | custom-call | tf_op jit(solution)/shard_map/pallas_call | solution.py:612
  73.5 0.6 copy.9
  74.1 0.6 copy.10
